TPU v7x, 16 devices: a whole 2x2x2 slice. The times are simulated.
16 devices in a mesh: col: 2 (over z), row: 8 (over y, x, core).
Axes of the slice: x: 2, y: 2, z: 2, core: 2. Of those that a mesh axis runs over, the one named last changes fastest.
Arguments:
- t_amps: float32 [2304, 9216], P('row', 'col')
- d_denom: float32 [2304, 9216], P('row', 'col')
- v_oovv: bfloat16 [2304, 9216], P('row', 'col')
- v_vvvv: bfloat16 [9216, 9216], P('row', 'col')
- v_oooo: bfloat16 [2304, 2304], replicated
- w_mixed: bfloat16 [4608, 4608], P(None, 'col')
Outputs:
- output: float32 [2304, 9216], P('row', 'col')
All inputs are finite; a program needn't handle non-finite values.
Results may differ from a plain program's by a relative error of at most 0.00139.
Values are sent between devices in bfloat16 or wider.
A program may use at most 1 GiB of HBM per device.

v0:
```python
import math
import jax
import jax.numpy as jnp
from jax import lax
from jax.sharding import PartitionSpec as P


def sweep_local(t_block, d_block, oovv_block, oovv_add, vvvv_block, oooo_cols, w_block, n_occ, n_vir, n_row, n_col):
    occ_here = n_occ // n_row
    vir_here = n_vir // n_col
    rows_here = occ_here * n_occ
    t_half = t_block.astype(jnp.bfloat16)
    t_rowfull = lax.all_gather(t_half, "col", axis=1, tiled=True)
    t_ladder = lax.all_to_all(t_rowfull, "row", 1, 0, tiled=True)
    ladder_part = jnp.dot(t_ladder, vvvv_block, preferred_element_type=jnp.float32)
    ladder = lax.psum_scatter(ladder_part, "row", scatter_dimension=0, tiled=True)
    t_colfull = lax.all_gather(t_half, "row", axis=0, tiled=True)
    inter_part = lax.dot_general(oovv_block, t_colfull, (((1,), (1,)), ((), ())), preferred_element_type=jnp.float32)
    inter_rows = lax.psum(inter_part, "col")
    inter_cols = lax.all_to_all(inter_rows, "row", 1, 0, tiled=True)
    hole_w = (oooo_cols + 0.5 * inter_cols).astype(jnp.bfloat16)
    hole_term = lax.dot_general(hole_w, t_colfull, (((0,), (0,)), ((), ())), preferred_element_type=jnp.float32)
    t_four = t_rowfull.reshape(occ_here, n_occ, n_vir, n_vir)
    w_three = w_block.reshape(n_occ, n_vir, w_block.shape[1])
    mix_part = jnp.einsum("ikac,kcn->ian", t_four, w_three, preferred_element_type=jnp.float32)
    mix_back = lax.all_to_all(mix_part, "col", 1, 2, tiled=True)
    mix_four = mix_back.reshape(occ_here, vir_here, n_occ, n_vir).transpose(0, 2, 1, 3)
    swap_rows = lax.all_to_all(mix_four, "row", 1, 0, tiled=True)
    swap_both = lax.all_to_all(swap_rows, "col", 3, 2, tiled=True)
    mix_sym = mix_four + swap_both.transpose(1, 0, 3, 2)
    resid_sum = oovv_add + ladder + hole_term + mix_sym.reshape(rows_here, vir_here * n_vir)
    return resid_sum / d_block


def solution(mesh):
    n_row = mesh.shape["row"]
    n_col = mesh.shape["col"]
    blk_spec = P("row", "col")

    def local_sweeps(t_block, d_block, oovv_block, vvvv_block, oooo_full, w_block):
        n_occ = math.isqrt(oooo_full.shape[0])
        n_vir = w_block.shape[0] // n_occ
        rows_here = oooo_full.shape[0] // n_row
        row_idx = lax.axis_index("row")
        oooo_cols = lax.dynamic_slice_in_dim(oooo_full, row_idx * rows_here, rows_here, axis=1).astype(jnp.float32)
        oovv_add = oovv_block.astype(jnp.float32)
        t_mid = sweep_local(t_block, d_block, oovv_block, oovv_add, vvvv_block, oooo_cols, w_block, n_occ, n_vir, n_row, n_col)
        return sweep_local(t_mid, d_block, oovv_block, oovv_add, vvvv_block, oooo_cols, w_block, n_occ, n_vir, n_row, n_col)

    return jax.shard_map(
        local_sweeps,
        mesh=mesh,
        in_specs=(blk_spec, blk_spec, blk_spec, blk_spec, P(), P(None, "col")),
        out_specs=blk_spec,
        check_vma=False,
    )
```

profile of v0, /device:TPU:0, one launch (start us, length us, event | category | flops | bytes accessed | tf_op | source)
XLA Modules:
  0.0 1723.5 jit_solution(4275880306945371411)
XLA Ops:
  11.6 70.1 %all-gather.5.cloned.1.call-done = bf16[288,9216]{1,0:T(8,128)(2,1)} async-done(((bf16[288,4608]{1,0:T(8,128)(2,1)}), bf16[288,9216]{1,0:T(8,128)(2,1)}) %all-gather.5.cloned.1.call-update) | async-done | bytes 5308432 | tf_op jit(solution)/shard_map/all_gather | solution.py:13
  92.0 152.3 %all-gather.7.cloned.1.call-done = bf16[2304,4608]{1,0:T(8,128)(2,1)} async-done(((bf16[288,4608]{1,0:T(8,128)(2,1)}), bf16[2304,4608]{1,0:T(8,128)(2,1)}) %all-gather.7.cloned.1.call-update) | async-done | bytes 21233680 | tf_op jit(solution)/shard_map/all_gather | solution.py:17
  263.0 34.7 %fusion.7 = f32[2304,4608]{1,0:T(8,128)} fusion(bf16[2304,1152]{1,0:T(8,128)(2,1)} %bitcast.1, bf16[1152,4608]{1,0:T(8,128)(2,1)} %param.9), kind=kOutput, calls=%fused_computation.26 | convolution fusion | flops 24461180928 | bytes 58392576 | tf_op jit(solution)/shard_map/dot_general | solution.py:15
  308.9 16.7 convolution_bitcast_fusion.1
  328.8 100.1 %all_to_all.166 = f32[6,96,2304]{2,0,1:T(8,128)S(1)} all-to-all(f32[6,96,2304]{2,0,1:T(8,128)S(1)} %copy.58), channel_id=1, replica_groups=mesh['col'=2,'row'=8] {'col'}, dimensions={1} | all-to-all | bytes 10616832 | tf_op jit(solution)/shard_map/all_to_all | solution.py:26
  449.3 151.7 %all_to_all.167 = f32[6,48,48,96]{3,2,0,1:T(8,128)S(1)} all-to-all(f32[6,48,48,96]{3,2,0,1:T(8,128)S(1)} %copy.60), channel_id=1, replica_groups=mesh['col'=2,'row'=8] {'row'}, dimensions={1} | all-to-all | bytes 10616832 | tf_op jit(solution)/shard_map/all_to_all | solution.py:28
  604.8 15.0 copy.63
  619.8 22.6 %reshape.50 = f32[2,1,663552]{2,1,0:T(1,128)} reshape(f32[96,6,48,48]{3,2,1,0:T(8,128)} %bitcast.99) | data formatting | bytes 10616832
  642.3 65.1 %all_to_all.168 = f32[2,1,663552]{2,1,0:T(1,128)} all-to-all(f32[2,1,663552]{2,1,0:T(1,128)} %reshape.50), channel_id=1, replica_groups=mesh['col'=2,'row'=8] {'col'}, dimensions={0} | all-to-all | bytes 10616832 | tf_op jit(solution)/shard_map/all_to_all | solution.py:29
  712.1 61.6 %reduce = f32[2,663552]{1,0:T(2,128)} reduce(f32[2,1,663552]{2,1,0:T(1,128)} %all_to_all.168, f32[]{:T(128)} %broadcast.13), dimensions={1}, to_apply=%all_to_all.135.reduce_sub_computation | reduce | bytes 10616836 | tf_op jit(solution)/shard_map/all_to_all | solution.py:29
  788.4 21.4 %copy.95 = f32[48,6,48,2,48]{2,3,0,4,1:T(2,128)} copy(f32[48,6,48,2,48]{2,0,1,4,3:T(8,128)} %bitcast.97) | data formatting | bytes 10616832 | tf_op jit(solution)/shard_map/all_to_all | solution.py:29
  848.3 17.0 fusion.4
  865.9 67.9 %all-gather.9.cloned.1.call-done = bf16[288,9216]{1,0:T(8,128)(2,1)} async-done(((bf16[288,4608]{1,0:T(8,128)(2,1)}), bf16[288,9216]{1,0:T(8,128)(2,1)}) %all-gather.9.cloned.1.call-update) | async-done | bytes 5308432 | tf_op jit(solution)/shard_map/all_gather | solution.py:13
  943.8 152.4 %all-gather.11.cloned.1.call-done = bf16[2304,4608]{1,0:T(8,128)(2,1)} async-done(((bf16[288,4608]{1,0:T(8,128)(2,1)}), bf16[2304,4608]{1,0:T(8,128)(2,1)}) %all-gather.11.cloned.1.call-update) | async-done | bytes 21233680 | tf_op jit(solution)/shard_map/all_gather | solution.py:17
  1114.8 34.9 %fusion.9 = f32[2304,4608]{1,0:T(8,128)} fusion(bf16[2304,1152]{1,0:T(8,128)(2,1)} %bitcast.20, bf16[1152,4608]{1,0:T(8,128)(2,1)} %param.9), kind=kOutput, calls=%fused_computation.28 | convolution fusion | flops 24461180928 | bytes 58392576 | tf_op jit(solution)/shard_map/dot_general | solution.py:15
  1160.9 16.7 convolution_bitcast_fusion
  1180.8 100.1 %all_to_all.169 = f32[6,96,2304]{2,0,1:T(8,128)S(1)} all-to-all(f32[6,96,2304]{2,0,1:T(8,128)S(1)} %copy.69), channel_id=1, replica_groups=mesh['col'=2,'row'=8] {'col'}, dimensions={1} | all-to-all | bytes 10616832 | tf_op jit(solution)/shard_map/all_to_all | solution.py:26
  1301.3 151.6 %all_to_all.170 = f32[6,48,48,96]{3,2,0,1:T(8,128)S(1)} all-to-all(f32[6,48,48,96]{3,2,0,1:T(8,128)S(1)} %copy.71), channel_id=1, replica_groups=mesh['col'=2,'row'=8] {'row'}, dimensions={1} | all-to-all | bytes 10616832 | tf_op jit(solution)/shard_map/all_to_all | solution.py:28
  1456.7 15.0 copy.74
  1471.7 22.6 %reshape.52 = f32[2,1,663552]{2,1,0:T(1,128)} reshape(f32[96,6,48,48]{3,2,1,0:T(8,128)} %bitcast.101) | data formatting | bytes 10616832
  1494.2 65.1 %all_to_all.171 = f32[2,1,663552]{2,1,0:T(1,128)} all-to-all(f32[2,1,663552]{2,1,0:T(1,128)} %reshape.52), channel_id=1, replica_groups=mesh['col'=2,'row'=8] {'col'}, dimensions={0} | all-to-all | bytes 10616832 | tf_op jit(solution)/shard_map/all_to_all | solution.py:29
  1563.4 61.6 %reduce.1 = f32[2,663552]{1,0:T(2,128)} reduce(f32[2,1,663552]{2,1,0:T(1,128)} %all_to_all.171, f32[]{:T(128)} %broadcast.13), dimensions={1}, to_apply=%all_to_all.152.reduce_sub_computation | reduce | bytes 10616836 | tf_op jit(solution)/shard_map/all_to_all | solution.py:29
  1639.7 21.4 %copy.94 = f32[48,6,48,2,48]{2,3,0,4,1:T(2,128)} copy(f32[48,6,48,2,48]{2,0,1,4,3:T(8,128)} %bitcast.98) | data formatting | bytes 10616832 | tf_op jit(solution)/shard_map/all_to_all | solution.py:29
  1698.0 18.4 %fusion.2 = f32[288,4608]{1,0:T(8,128)} fusion(f32[288,4608]{1,0:T(8,128)} %param.7, f32[288,4608]{1,0:T(8,128)} %reshape.46, bf16[2304,288]{1,0:T(8,128)(2,1)S(1)} %fusion.6, bf16[2304,4608]{1,0:T(8,128)(2,1)} %all-gather.11.cloned.1.call-done, f32[288,4608]{1,0:T(8,128)} %reduce-scatter.5.cloned.1.call-done, bf16[288,4608]{1,0:T(8,128)(2,1)} %param.8), kind=kOutput, calls=%fused_computation.10 | convolution fusion | flops 6121930752 | bytes 46448640 | tf_op jit(solution)/shard_map/dot_general | solution.py:22
  (68 shorter events, 253.8 us)
Async XLA Ops:
  6.5 75.2 %all-gather.5.cloned.1.call-start = ((), (), s32[]{:S(2)}) async-start(), calls=%async_computation.12 | async-start | bytes 7962624 | tf_op jit(solution)/shard_map/all_gather | solution.py:13
  10.8 233.4 %all-gather.7.cloned.1.call-start = ((), (), s32[]{:S(2)}) async-start(), calls=%async_computation.14 | async-start | bytes 23887872 | tf_op jit(solution)/shard_map/all_gather | solution.py:17
  87.0 157.3 %copy-start = (bf16[288,4608]{1,0:T(8,128)(2,1)S(1)}, bf16[288,4608]{1,0:T(8,128)(2,1)}, u32[]{:S(2)}) copy-start(bf16[288,4608]{1,0:T(8,128)(2,1)} %param.8) | copy-start | bytes 7962628
  87.0 176.0 %all-to-all-start = ((bf16[288,8,1152]{2,0,1:T(8,128)(2,1)}), bf16[288,8,1152]{2,0,1:T(8,128)(2,1)}, u32[]{:S(2)}, u32[]{:S(2)}) async-start(bf16[288,8,1152]{2,0,1:T(8,128)(2,1)} %bitcast.109), calls=%async_computation | async-start | bytes 10616832 | tf_op jit(solution)/shard_map/all_to_all | solution.py:14
  91.9 615.5 %all-reduce.3.cloned.1.call-start = ((), (), s32[]{:S(2)}) async-start(), calls=%async_computation.15 | async-start | bytes 7077888 | tf_op jit(solution)/shard_map/psum | solution.py:19
  262.7 585.6 %reduce-scatter.3.cloned.1.call-start = ((), (), s32[]{:S(2)}) async-start(), calls=%async_computation.13 | async-start | bytes 47775744 | tf_op jit(solution)/shard_map/reduce_scatter | solution.py:16
  707.4 136.0 %all-to-all-start.1 = ((f32[288,8,288]{2,0,1:T(8,128)}), f32[288,8,288]{2,0,1:T(8,128)S(1)}, u32[]{:S(2)}, u32[]{:S(2)}) async-start(f32[288,8,288]{2,0,1:T(8,128)} %all-reduce.3.cloned.1.call-done), calls=%async_computation.2 | async-start | bytes 7077888 | tf_op jit(solution)/shard_map/all_to_all | solution.py:20
  711.1 222.8 %all-gather.9.cloned.1.call-start = ((), (), s32[]{:S(2)}) async-start(), calls=%async_computation.16 | async-start | bytes 7962624 | tf_op jit(solution)/shard_map/all_gather | solution.py:13
  843.6 4.7 copy-start.1
  865.4 230.9 %all-gather.11.cloned.1.call-start = ((), (), s32[]{:S(2)}) async-start(), calls=%async_computation.18 | async-start | bytes 23887872 | tf_op jit(solution)/shard_map/all_gather | solution.py:17
  939.1 175.7 %all-to-all-start.5 = ((bf16[288,8,1152]{2,0,1:T(8,128)(2,1)}), bf16[288,8,1152]{2,0,1:T(8,128)(2,1)}, u32[]{:S(2)}, u32[]{:S(2)}) async-start(bf16[288,8,1152]{2,0,1:T(8,128)(2,1)} %bitcast.110), calls=%async_computation.6 | async-start | bytes 10616832 | tf_op jit(solution)/shard_map/all_to_all | solution.py:14
  943.8 615.5 %all-reduce.5.cloned.1.call-start = ((), (), s32[]{:S(2)}) async-start(), calls=%async_computation.19 | async-start | bytes 7077888 | tf_op jit(solution)/shard_map/psum | solution.py:19
  1114.8 583.3 %reduce-scatter.5.cloned.1.call-start = ((), (), s32[]{:S(2)}) async-start(), calls=%async_computation.17 | async-start | bytes 47775744 | tf_op jit(solution)/shard_map/reduce_scatter | solution.py:16
  1559.3 135.2 %all-to-all-start.6 = ((f32[288,8,288]{2,0,1:T(8,128)}), f32[288,8,288]{2,0,1:T(8,128)S(1)}, u32[]{:S(2)}, u32[]{:S(2)}) async-start(f32[288,8,288]{2,0,1:T(8,128)} %all-reduce.5.cloned.1.call-done), calls=%async_computation.8 | async-start | bytes 7077888 | tf_op jit(solution)/shard_map/all_to_all | solution.py:20
Sparse Core Ops, SparseCore 0:
  11.0 70.6 all-gather.4
  83.5 160.6 all-gather.6
  262.9 108.6 all-reduce.2
  375.0 317.8 reduce-scatter.2
  865.5 68.2 all-gather.8
  935.5 160.6 all-gather.10
  1114.9 108.6 all-reduce.4
  1227.1 317.8 reduce-scatter.4
where the time goes:
time: 1730 us; the launch traced here: 1720 us
  blocking collectives  634 us (37%)
  waiting for transfers between devices  444 us (26%)
  local copies, waits for them, and re-layouts  303 us (18%)
  matrix products  163 us (9%)
  other arithmetic  148 us (9%)
  starting transfers between devices  18.3 us (1%)
    all_gather x2, waiting for transfers between devices, sweep_local(): t_colfull = lax.all_gather(t_half, 'row', axis=0, tiled=True)  305 us
    all_to_all x2, blocking collectives, sweep_local(): swap_rows = lax.all_to_all(mix_four, 'row', 1, 0, tiled=True)  303 us
    all_to_all x2, blocking collectives, sweep_local(): mix_back = lax.all_to_all(mix_part, 'col', 1, 2, tiled=True)  200 us
    all_gather x2, waiting for transfers between devices, sweep_local(): t_rowfull = lax.all_gather(t_half, 'col', axis=1, tiled=True)  138 us
    all_to_all x2, blocking collectives, sweep_local(): swap_both = lax.all_to_all(swap_rows, 'col', 3, 2, tiled=True)  130 us
    all_to_all x2, other arithmetic, sweep_local(): swap_both = lax.all_to_all(swap_rows, 'col', 3, 2, tiled=True)  123 us
    unnamed x8, local copies, waits for them, and re-layouts  74.3 us
    all_to_all x5, local copies, waits for them, and re-layouts, sweep_local(): swap_both = lax.all_to_all(swap_rows, 'col', 3, 2, tiled=True)  71.8 us
  transfers between devices with their start and end apart: 12, of which 4 were waited for; matrix products, arithmetic and copies ran while one was open for 31% of the time, Pallas kernels for 0%

commit v1 on v0

v1 whole, which is shorter than its diff:
```python
import functools
import math
import jax
import jax.numpy as jnp
from jax import lax
from jax.experimental import pallas as pl
from jax.experimental.pallas import tpu as pltpu
from jax.sharding import PartitionSpec as P


X_BIT, Y_BIT, CORE_BIT = 2, 4, 1
N_CHUNK = 3
F32 = jnp.float32
BF16 = jnp.bfloat16


def swap_row(value, bit):
    return lax.ppermute(value, "row", [(i, i ^ bit) for i in range(8)])


def swap_col(value):
    return lax.ppermute(value, "col", [(0, 1), (1, 0)])


def mm(lhs, rhs, dims=(((1,), (0,)), ((), ()))):
    return lax.dot_general(lhs, rhs, dims, preferred_element_type=F32)


def pick(flag, if_true, if_false):
    return jnp.where(flag, if_true, if_false)


def cut(value, k, size, axis):
    return lax.dynamic_slice_in_dim(value, k * size, size, axis=axis)


def split_cols(value, n):
    width = value.shape[1] // (2 * n)
    cols = [lax.slice_in_dim(value, k * width, (k + 1) * width, axis=1) for k in range(2 * n)]
    return [jnp.concatenate([cols[k], cols[n + k]], axis=1) for k in range(n)]


def join_cols(parts):
    width = parts[0].shape[1] // 2
    return jnp.concatenate([p[:, :width] for p in parts] + [p[:, width:] for p in parts], axis=1)


def order_columns(w, n_vir):
    half = n_vir // 2
    group = 8 * n_vir
    src = jnp.arange(group)
    j, rest = src // n_vir, src % n_vir
    dst = (rest // half) * (8 * half) + j * half + rest % half
    perm = (dst[:, None] == jnp.arange(group)[None, :]).astype(BF16)
    parts = [mm(lax.slice_in_dim(w, g, g + group, axis=1), perm).astype(BF16) for g in range(0, w.shape[1], group)]
    lo = [p[:, : group // 2] for p in parts]
    hi = [p[:, group // 2 :] for p in parts]
    return jnp.concatenate(lo + hi, axis=1)


def fold_kernel(occ_l, vir_l, n_occ, n_vir, pos_ref, own_ref, oth_ref, s_ref, out_ref, buf):
    half = own_ref.shape[1] // 2
    blk = occ_l * vir_l
    x, c, z = pos_ref[0], pos_ref[1], pos_ref[2]
    stride = buf.shape[0] // vir_l
    pad = jnp.zeros((vir_l, buf.shape[1] - n_vir), F32)
    for yy in range(2):
        near, far = (own_ref, oth_ref) if yy == 0 else (oth_ref, own_ref)
        for xx in range(2):
            for cc in range(2):
                s_idx = lax.bitwise_xor(x, xx) * 2 + lax.bitwise_xor(c, cc)
                for jl in range(occ_l):
                    j = ((yy * 2 + xx) * 2 + cc) * occ_l + jl
                    both = []
                    for zz in range(2):
                        m_off = zz * half + (xx * 2 + cc) * blk + jl * vir_l
                        s_off = (yy * 2 + zz) * blk + jl * vir_l
                        m = jnp.where(z == 0, near[:, m_off : m_off + vir_l], far[:, m_off : m_off + vir_l])
                        both.append(m + s_ref[s_idx, :, s_off : s_off + vir_l])
                    buf[pl.ds(j, vir_l, stride=stride), :] = jnp.concatenate(both + [pad], axis=1)
    for a in range(vir_l):
        out_ref[:, a * n_vir : (a + 1) * n_vir] = buf[a * stride : a * stride + n_occ, :n_vir]


def fold(pos, own, oth, s_all, occ_l, vir_l, n_occ, n_vir):
    width = own.shape[1]
    return pl.pallas_call(
        functools.partial(fold_kernel, occ_l, vir_l, n_occ, n_vir),
        grid=(occ_l,),
        out_shape=jax.ShapeDtypeStruct((occ_l * n_occ, vir_l * n_vir), F32),
        in_specs=[
            pl.BlockSpec(memory_space=pltpu.SMEM),
            pl.BlockSpec((vir_l, width), lambda i: (i, 0)),
            pl.BlockSpec((vir_l, width), lambda i: (i, 0)),
            pl.BlockSpec((4, vir_l, s_all.shape[2]), lambda i: (0, i, 0)),
        ],
        out_specs=pl.BlockSpec((n_occ, vir_l * n_vir), lambda i: (i, 0)),
        scratch_shapes=[pltpu.VMEM((vir_l * (n_occ + 8), 128), F32)],
        cost_estimate=pl.CostEstimate(flops=20_000_000_000, bytes_accessed=16_000_000, transcendentals=0),
        name="fold",
    )(pos, own, oth, s_all)


def ladder_kernel(pos_ref, lhs_ref, v0, v1, v2, v3, w_ref, k0, k1, k2, k3, away_ref, home_ref):
    depth = v0.shape[0]
    acc = None
    for p, v in enumerate((v0, v1, v2, v3)):
        off = pl.multiple_of(pos_ref[p] * depth, 128)
        term = jnp.dot(lhs_ref[:, pl.ds(off, depth)], v[...], preferred_element_type=F32)
        acc = term if acc is None else acc + term
    rows = k0.shape[0]
    for p, k in enumerate((k0, k1, k2, k3)):
        acc = acc + jnp.dot(w_ref[:, p * rows : (p + 1) * rows], k[...], preferred_element_type=F32)
    half = away_ref.shape[0]
    away_ref[...] = acc[:half]
    home_ref[...] = acc[half:]


def ladder(pos, lhs, v, w, k, tile):
    m, n = lhs.shape[0], v[0].shape[1]

    def full(a):
        return pl.BlockSpec(a.shape, lambda i: (0, 0), pipeline_mode=pl.Buffered(1))

    def cols(rows):
        return pl.BlockSpec((rows, tile), lambda i: (0, i))

    out = jax.ShapeDtypeStruct((m // 2, n), F32)
    return pl.pallas_call(
        ladder_kernel,
        grid=(n // tile,),
        out_shape=(out, out),
        in_specs=[pl.BlockSpec(memory_space=pltpu.SMEM), full(lhs)]
        + [cols(a.shape[0]) for a in v]
        + [full(w)]
        + [cols(a.shape[0]) for a in k],
        out_specs=(cols(m // 2), cols(m // 2)),
        cost_estimate=pl.CostEstimate(
            flops=2 * m * n * (lhs.shape[1] + w.shape[1]), bytes_accessed=24_000_000, transcendentals=0
        ),
        name="ladder",
    )(pos, lhs, *v, w, *k)


def flip_kernel(pos_ref, a0, a1, a2, a3, out_ref, buf):
    rows = a0.shape[0]
    for p, a in enumerate((a0, a1, a2, a3)):
        buf[pl.ds(pl.multiple_of(pos_ref[p] * rows, 8), rows), :] = a[...]
    out_ref[...] = buf[...].T


def flip(pos, arrays, tile):
    rows, n = arrays[0].shape
    return pl.pallas_call(
        flip_kernel,
        grid=(n // tile,),
        out_shape=jax.ShapeDtypeStruct((n, 4 * rows), F32),
        in_specs=[pl.BlockSpec(memory_space=pltpu.SMEM)] + [pl.BlockSpec((rows, tile), lambda i: (0, i))] * 4,
        out_specs=pl.BlockSpec((tile, 4 * rows), lambda i: (i, 0)),
        scratch_shapes=[pltpu.VMEM((4 * rows, tile), F32)],
        cost_estimate=pl.CostEstimate(flops=8_000_000_000, bytes_accessed=11_000_000, transcendentals=0),
        name="flip",
    )(pos, *arrays)


def finish_kernel(pos_ref, oovv_ref, home_ref, got_ref, mix_ref, d_ref, out_ref, near_ref=None):
    total = oovv_ref[...].astype(F32) + (home_ref[...] + got_ref[...]) + mix_ref[...]
    total = (total / d_ref[...]).astype(out_ref.dtype)
    out_ref[...] = total
    if near_ref is not None:

        @pl.when(pl.program_id(0) == pos_ref[0])
        def _():
            near_ref[...] = total


def finish(n, pos, oovv, home, got, mixed, d, dtype):
    rows, width = home.shape
    steps = 2
    tile = width // steps
    whole = pl.BlockSpec((rows, tile), lambda i: (0, n + N_CHUNK * i))
    part = pl.BlockSpec((rows, tile), lambda i: (0, i))
    out_shape = [jax.ShapeDtypeStruct((rows, width), dtype)]
    out_specs = [part]
    if dtype == BF16:
        out_shape.append(jax.ShapeDtypeStruct((rows, tile), dtype))
        out_specs.append(pl.BlockSpec((rows, tile), lambda i: (0, 0)))
    return pl.pallas_call(
        finish_kernel,
        grid=(steps,),
        out_shape=out_shape,
        in_specs=[pl.BlockSpec(memory_space=pltpu.SMEM), whole, part, part, whole, whole],
        out_specs=out_specs,
        cost_estimate=pl.CostEstimate(flops=3_000_000_000, bytes_accessed=9_000_000, transcendentals=0),
        name="finish",
    )(pos, oovv, home, got, mixed, d)


def mixed_product(t_four, w):
    out = jnp.einsum("ikac,kcn->ian", t_four, w, preferred_element_type=F32)
    return out.reshape(out.shape[0] * out.shape[1], -1)


def after(value, *deps):
    return lax.optimization_barrier((value, *deps))[0]


def solution(mesh):
    blk_spec = P("row", "col")

    def local_sweeps(t_block, d_block, oovv_block, vvvv_block, oooo_full, w_block):
        n_occ = math.isqrt(oooo_full.shape[0])
        n_vir = w_block.shape[0] // n_occ
        rows, cols = t_block.shape
        occ_l = n_occ // 8
        vir_l = n_vir // 2
        row = lax.axis_index("row")
        z = lax.axis_index("col")
        y, x, c = row // 4, (row // 2) % 2, row % 2
        y_is_z = y == z
        pos_fold = jnp.stack([x, c, z]).astype(jnp.int32)
        pos_ladder = jnp.stack([((y ^ dy) ^ z) * 2 + (c ^ dc) for dy, dc in ((0, 0), (1, 0), (0, 1), (1, 1))])
        pos_ladder = pos_ladder.astype(jnp.int32)

        pos_flip = jnp.stack([2 * (y ^ dy) + (z ^ dz) for dy, dz in ((0, 0), (0, 1), (1, 0), (1, 1))])
        pos_flip = pos_flip.astype(jnp.int32)

        quarter = w_block.shape[0] // 4
        piece = quarter // 2
        w_sends = [
            order_columns(lax.dynamic_slice_in_dim(w_block, (2 * x + c) * quarter + s * piece, piece, axis=0), n_vir)
            for s in range(2)
        ]
        t_first = split_cols(after(t_block, *w_sends).astype(BF16), N_CHUNK)
        w_oth = jnp.zeros(w_block.shape, BF16)
        for s in range(2):
            w_got = swap_col(w_sends[s])
            w_far = swap_row(w_got, X_BIT)
            w_q = [w_got, swap_row(w_got, CORE_BIT), w_far, swap_row(w_far, CORE_BIT)]
            for m in range(4):
                start = ((2 * x + c) ^ m) * quarter + s * piece
                w_oth = lax.dynamic_update_slice_in_dim(w_oth, w_q[m], start, axis=0)
        w_own = order_columns(after(w_block, *t_first), n_vir)
        w_own = w_own.reshape(n_occ, n_vir, w_own.shape[1])
        w_oth = w_oth.reshape(n_occ, n_vir, w_oth.shape[1])

        oovv_y = swap_row(oovv_block, Y_BIT)
        oovv_set = jnp.concatenate(
            [oovv_block, swap_row(oovv_block, CORE_BIT), oovv_y, swap_row(oovv_y, CORE_BIT)], axis=0
        )
        oooo_rows = jnp.concatenate([cut(oooo_full, row ^ m, rows, 0) for m in (0, 1, 4, 5)], axis=0)
        oooo_half = cut(oooo_rows, row ^ (X_BIT * (1 - z)), rows, 1).T.astype(F32)

        v_near = split_cols(after(vvvv_block, *t_first), N_CHUNK)
        v_set = [None] * N_CHUNK

        def fetch_v(n, part):
            part_y = swap_row(part, Y_BIT)
            v_set[n] = [part, part_y, swap_row(part, CORE_BIT), swap_row(part_y, CORE_BIT)]

        def near_half(p):
            wide = p.shape[1] // 2
            return pick(x == 0, p[:, :wide], p[:, wide:])

        def sweep(t_parts, near_parts, last):
            t_x = [swap_row(p, X_BIT) for p in t_parts]
            t_y = [swap_row(p, Y_BIT) for p in t_parts]
            t_c = [swap_row(p, CORE_BIT) for p in t_parts]
            t_yc = [swap_row(p, CORE_BIT) for p in t_y]
            t_full = join_cols(t_parts)
            tx_full = join_cols(t_x)

            def far(send):
                return jnp.concatenate([swap_col(p) for p in send], axis=1)

            t_rows = jnp.concatenate([tx_full, t_full], axis=0)
            if not last:
                for n in range(N_CHUNK - 1):
                    fetch_v(n, v_near[n])

            t_four = t_full.reshape(occ_l, n_occ, vir_l, n_vir)
            mix_own = mixed_product(t_four, w_own)
            far_own = far(near_parts)

            if last:
                mix_oth = mixed_product(t_four, w_oth)
                t_rows = after(t_rows, mix_oth)
            inter = mm(t_rows, oovv_set, (((1,), (1,)), ((), ())))
            inter_send = cut(inter, 1 - z, rows, 0)
            inter_sum = cut(inter, z, rows, 0) + swap_col(inter_send)
            hole_half = (oooo_half + 0.5 * inter_sum).astype(BF16)
            hole_got = swap_col(hole_half)
            hole_w = jnp.concatenate([pick(z == 0, hole_half, hole_got), pick(z == 0, hole_got, hole_half)], axis=0)

            near_x = [near_half(p) for p in t_x[:-1]]
            near_x.append(near_half(after(t_x[-1], *near_x)))
            far_x = far(near_x)
            near = cut(t_rows, x, cols // 2, 1)
            lhs = jnp.concatenate([near, jnp.concatenate([far_x, far_own], axis=0)], axis=1)

            if not last:
                t_late = after(t_four, hole_half)
                mix_oth = mixed_product(t_late, w_oth)

            half_w = mix_own.shape[1] // 2
            keep_own, keep_oth = cut(mix_own, z, half_w, 1), cut(mix_oth, z, half_w, 1)
            give_own, give_oth = cut(mix_own, 1 - z, half_w, 1), cut(mix_oth, 1 - z, half_w, 1)
            got_away = swap_col(pick(y_is_z, give_oth, give_own))
            got_here = swap_col(pick(y_is_z, give_own, give_oth))
            send0 = pick(y_is_z, keep_oth, keep_own)

            def ladder_part(n):
                k_rows = (t_parts[n], t_c[n], t_y[n], t_yc[n])
                away, home = ladder(pos_ladder, lhs, v_set[n], hole_w, k_rows, 512)
                return away, home, swap_row(away, X_BIT)

            here = pick(y_is_z, keep_own, keep_oth)
            away0, away1 = swap_row(send0, Y_BIT), swap_row(got_away, Y_BIT)
            terms = [None] * N_CHUNK
            if not last:
                fetch_v(N_CHUNK - 1, after(v_near[-1], send0, got_away))
                for n in range(N_CHUNK - 1):
                    terms[n] = ladder_part(n)
                here = after(here, *[t[0] for t in terms[:-1]])
            flipped = flip(pos_flip, (here, got_here, away0, away1), 384)
            by_x = [cut(flipped, x, 2 * rows, 0), swap_row(cut(flipped, 1 - x, 2 * rows, 0), X_BIT)]
            s_all = []
            for f in by_x:
                s_all += [cut(f, c, rows, 0), swap_row(cut(f, 1 - c, rows, 0), CORE_BIT)]
            s_all = jnp.stack(s_all)
            mixed = fold(pos_fold, mix_own, mix_oth, s_all, occ_l, vir_l, n_occ, n_vir)

            def close(n):
                _, home, got = terms[n]
                return finish(n, pos_fold, oovv_block, home, got, mixed, d_block, F32 if last else BF16)

            for n in range(N_CHUNK):
                if terms[n] is None:
                    terms[n] = ladder_part(n)
            return [close(n) for n in range(N_CHUNK)]

        mid = sweep(t_first, [near_half(p) for p in t_first], False)
        final = sweep([p[0] for p in mid], [p[1] for p in mid], True)
        return join_cols([p[0] for p in final])

    return jax.shard_map(
        local_sweeps,
        mesh=mesh,
        in_specs=(blk_spec, blk_spec, blk_spec, blk_spec, P(), P(None, "col")),
        out_specs=blk_spec,
        check_vma=False,
    )
```

time: 1730 us -> 1340 us (0.77)
  blocking collectives: 634 us -> 0 us
  waiting for transfers between devices: 444 us -> 701 us
  Pallas kernels: 0 us -> 214 us
  local copies, waits for them, and re-layouts: 303 us -> 167 us
  other arithmetic: 148 us -> 80 us
  matrix products: 163 us -> 104 us
  starting transfers between devices: 18.3 us -> 63.1 us
    ppermute x0 -> x80, waiting for transfers between devices: none -> 701 us  [the longest x58 533 us: swap_row(): return lax.ppermute(value, 'row', [(i, i ^ bit) for i in range(8)])]
    all_to_all x6 -> x0, blocking collectives: 634 us -> none  [the longest x2 303 us: sweep_local(): swap_rows = lax.all_to_all(mix_four, 'row', 1, 0, tiled=True)]
    all_gather x4 -> x0, waiting for transfers between devices: 443 us -> none  [the longest x2 305 us: sweep_local(): t_colfull = lax.all_gather(t_half, 'row', axis=0, tiled=True)]
    pallas_call x0 -> x16, Pallas kernels: none -> 214 us  [the longest x6 119 us: ladder(): pl.pallas_call(ladder_kernel, grid=(n // tile,), out_shape=(out, out), in...]
    all_to_all x17 -> x0, local copies, waits for them, and re-layouts: 146 us -> none  [the longest x5 71.8 us: sweep_local(): swap_both = lax.all_to_all(swap_rows, 'col', 3, 2, tiled=True)]
    all_to_all x2 -> x0, other arithmetic: 123 us -> none  [sweep_local(): swap_both = lax.all_to_all(swap_rows, 'col', 3, 2, tiled=True)]
    ppermute x0 -> x80, starting transfers between devices: none -> 63.1 us  [the longest x58 33.5 us: swap_row(): return lax.ppermute(value, 'row', [(i, i ^ bit) for i in range(8)])]
    dot_general x8 -> x15, matrix products: 163 us -> 104 us  [the longest x11 59.7 us: mm(): return lax.dot_general(lhs, rhs, dims, preferred_element_type=F32)]
  transfers between devices with their start and end apart: 12 -> 80, of which waited for: 4 -> 27; matrix products, arithmetic and copies ran while one was open for 31% -> 25% of each run, Pallas kernels for 0% -> 15%
where the time goes in v1:
time: 1340 us; the launch traced here: 1330 us
  waiting for transfers between devices  701 us (52%)
  Pallas kernels  214 us (16%)
  local copies, waits for them, and re-layouts  167 us (12%)
  matrix products  104 us (8%)
  other arithmetic  80 us (6%)
  starting transfers between devices  63.1 us (5%)
    ppermute x58, waiting for transfers between devices, swap_row(): return lax.ppermute(value, 'row', [(i, i ^ bit) for i in range(8)])  533 us
    ppermute x22, waiting for transfers between devices, swap_col(): return lax.ppermute(value, 'col', [(0, 1), (1, 0)])  167 us
    pallas_call x6, Pallas kernels, ladder(): pl.pallas_call(ladder_kernel, grid=(n // tile,), out_shape=(out, out), in...  119 us
    unnamed x164, local copies, waits for them, and re-layouts  62.1 us
    dot_general x11, matrix products, mm(): return lax.dot_general(lhs, rhs, dims, preferred_element_type=F32)  59.7 us
    pallas_call x2, Pallas kernels, fold(): pl.pallas_call(functools.partial(fold_kernel, occ_l, vir_l, n_occ, n_vir)...  54.2 us
    dot_general x4, matrix products, mixed_product(): out = jnp.einsum('ikac,kcn->ian', t_four, w, preferred_element_type=F32)  44.5 us
    ppermute x58, starting transfers between devices, swap_row(): return lax.ppermute(value, 'row', [(i, i ^ bit) for i in range(8)])  33.5 us
  transfers between devices with their start and end apart: 80, of which 27 were waited for; matrix products, arithmetic and copies ran while one was open for 25% of the time, Pallas kernels for 15%

profile of v1, /device:TPU:0, one launch (start us, length us, event | category | flops | bytes accessed | tf_op | source)
XLA Modules:
  0.0 1330.1 jit_solution(969935265905898698)
XLA Ops:
  87.9 26.7 %copy.21 = bf16[4608,2304]{1,0:T(8,128)(2,1)} copy(bf16[4608,2304]{0,1:T(8,128)(2,1)} %slice_dynamic-update-slice_fusion) | data formatting | bytes 42467328 | tf_op jit(solution)/shard_map/concatenate | solution.py:58
  190.1 28.5 %collective-permute-done.25 = bf16[576,2304]{1,0:T(8,128)(2,1)} collective-permute-done((bf16[576,2304]{1,0:T(8,128)(2,1)}, bf16[576,2304]{1,0:T(8,128)(2,1)}, u32[]{:S(2)}, u32[]{:S(2)}) %collective-permute-start.25) | collective-permute-done | bytes 2654240 | tf_op jit(solution)/shard_map/ppermute | solution.py:22
  224.0 19.7 %collective-permute-done.23 = bf16[576,2304]{1,0:T(8,128)(2,1)} collective-permute-done((bf16[576,2304]{1,0:T(8,128)(2,1)}, bf16[576,2304]{1,0:T(8,128)(2,1)}, u32[]{:S(2)}, u32[]{:S(2)}) %collective-permute-start.23) | collective-permute-done | bytes 2654240 | tf_op jit(solution)/shard_map/ppermute | solution.py:18
  258.7 40.0 %collective-permute-done.27 = bf16[576,2304]{1,0:T(8,128)(2,1)} collective-permute-done((bf16[576,2304]{1,0:T(8,128)(2,1)}, bf16[576,2304]{1,0:T(8,128)(2,1)}, u32[]{:S(2)}, u32[]{:S(2)}) %collective-permute-start.27) | collective-permute-done | bytes 2654240 | tf_op jit(solution)/shard_map/ppermute | solution.py:18
  371.5 62.1 %collective-permute-done.9.v1 = bf16[1152,1536]{1,0:T(8,128)(2,1)} collective-permute-done((bf16[1152,1536]{1,0:T(8,128)(2,1)}, bf16[1152,1536]{1,0:T(8,128)(2,1)}, u32[]{:S(2)}, u32[]{:S(2)}) %collective-permute-start.9) | collective-permute-done | bytes 3538976 | tf_op jit(solution)/shard_map/ppermute | solution.py:18
  438.7 69.4 %collective-permute-done.29.v1 = bf16[1152,1536]{1,0:T(8,128)(2,1)} collective-permute-done((bf16[1152,1536]{1,0:T(8,128)(2,1)}, bf16[1152,1536]{1,0:T(8,128)(2,1)}, u32[]{:S(2)}, u32[]{:S(2)}) %collective-permute-start.29) | collective-permute-done | bytes 3538976 | tf_op jit(solution)/shard_map/ppermute | solution.py:18
  514.8 23.5 %collective-permute-done.37 = f32[288,1152]{1,0:T(8,128)} collective-permute-done((f32[288,1152]{1,0:T(8,128)}, f32[288,1152]{1,0:T(8,128)}, u32[]{:S(2)}, u32[]{:S(2)}) %collective-permute-start.37) | collective-permute-done | bytes 1327136 | tf_op jit(solution)/shard_map/ppermute | solution.py:22
  560.6 19.9 %ladder.6 = (f32[288,1536]{1,0:T(8,128)}, f32[288,1536]{1,0:T(8,128)}) custom-call(s32[4]{0:T(128)} %pad_add_fusion.1.pos_ref, bf16[576,4608]{1,0:T(8,128)(2,1)} %maximum_maximum_fusion.lhs_ref, bf16[1152,1536]{1,0:T(8,128)(2,1)} %pad_maximum_fusion.5.v0, bf16[1152,1536]{1,0:T(8,128)(2,1)} %collective-permute-done.9.v1, ...), custom_call_target="tpu_custom_call" | custom-call | flops 10192158720 | bytes 24000000 | tf_op jit(solution)/shard_map/ladder/pallas_call | solution.py:129
  580.5 19.8 %ladder.7 = (f32[288,1536]{1,0:T(8,128)}, f32[288,1536]{1,0:T(8,128)}) custom-call(s32[4]{0:T(128)} %pad_add_fusion.1.pos_ref, bf16[576,4608]{1,0:T(8,128)(2,1)} %maximum_maximum_fusion.lhs_ref, bf16[1152,1536]{1,0:T(8,128)(2,1)} %pad_maximum_fusion.6.v0, bf16[1152,1536]{1,0:T(8,128)(2,1)} %collective-permute-done.29.v1, ...), custom_call_target="tpu_custom_call" | custom-call | flops 10192158720 | bytes 24000000 | tf_op jit(solution)/shard_map/ladder/pallas_call | solution.py:129
  600.3 92.2 %collective-permute-done.38.a3 = f32[288,1152]{1,0:T(8,128)} collective-permute-done((f32[288,1152]{1,0:T(8,128)}, f32[288,1152]{1,0:T(8,128)}, u32[]{:S(2)}, u32[]{:S(2)}) %collective-permute-start.38) | collective-permute-done | bytes 1327136 | tf_op jit(solution)/shard_map/ppermute | solution.py:18
  706.6 55.4 %collective-permute-done.40 = f32[576,1152]{1,0:T(8,128)} collective-permute-done((f32[576,1152]{1,0:T(8,128)}, f32[576,1152]{1,0:T(8,128)}, u32[]{:S(2)}, u32[]{:S(2)}) %collective-permute-start.40) | collective-permute-done | bytes 2654240 | tf_op jit(solution)/shard_map/ppermute | solution.py:18
  764.4 21.6 %collective-permute-done.49.k2 = bf16[288,1536]{1,0:T(8,128)(2,1)S(1)} collective-permute-done((bf16[288,1536]{1,0:T(8,128)(2,1)S(1)}, bf16[288,1536]{1,0:T(8,128)(2,1)S(1)}, u32[]{:S(2)}, u32[]{:S(2)}) %collective-permute-start.49) | collective-permute-done | bytes 884768 | tf_op jit(solution)/shard_map/ppermute | solution.py:18
  792.8 19.8 %ladder.8 = (f32[288,1536]{1,0:T(8,128)}, f32[288,1536]{1,0:T(8,128)}) custom-call(s32[4]{0:T(128)} %pad_add_fusion.1.pos_ref, bf16[576,4608]{1,0:T(8,128)(2,1)} %maximum_maximum_fusion.lhs_ref, bf16[1152,1536]{1,0:T(8,128)(2,1)} %pad_maximum_fusion.7.v0, bf16[1152,1536]{1,0:T(8,128)(2,1)} %collective-permute-done.45.v1, ...), custom_call_target="tpu_custom_call" | custom-call | flops 10192158720 | bytes 24000000 | tf_op jit(solution)/shard_map/ladder/pallas_call | solution.py:129
  814.1 27.1 %fold.2.mix_ref = f32[288,4608]{1,0:T(8,128)} custom-call(s32[3]{0:T(128)} %pad_add_fusion.pos_ref, f32[288,2304]{1,0:T(8,128)} %convolution_bitcast_fusion.3.own_ref, f32[288,2304]{1,0:T(8,128)} %convolution_bitcast_fusion.2.oth_ref, f32[4,288,1152]{2,1,0:T(8,128)} %pad_maximum_fusion.2.s_ref), custom_call_target="tpu_custom_call" | custom-call | flops 20000000000 | bytes 16000000 | tf_op jit(solution)/shard_map/fold/pallas_call | solution.py:87
  841.2 25.6 %collective-permute-done.20.got_ref = f32[288,1536]{1,0:T(8,128)} collective-permute-done((f32[288,1536]{1,0:T(8,128)}, f32[288,1536]{1,0:T(8,128)}, u32[]{:S(2)}, u32[]{:S(2)}) %collective-permute-start.20) | collective-permute-done | bytes 1769504 | tf_op jit(solution)/shard_map/ppermute | solution.py:18
  881.6 42.0 %collective-permute-done.42 = bf16[288,1536]{1,0:T(8,128)(2,1)S(1)} collective-permute-done((bf16[288,1536]{1,0:T(8,128)(2,1)}, bf16[288,1536]{1,0:T(8,128)(2,1)S(1)}, u32[]{:S(2)}, u32[]{:S(2)}) %collective-permute-start.42) | collective-permute-done | bytes 884768 | tf_op jit(solution)/shard_map/ppermute | solution.py:18
  1029.6 24.2 %collective-permute-done.59 = f32[288,1152]{1,0:T(8,128)S(1)} collective-permute-done((f32[288,1152]{1,0:T(8,128)S(1)}, f32[288,1152]{1,0:T(8,128)S(1)}, u32[]{:S(2)}, u32[]{:S(2)}) %collective-permute-start.59) | collective-permute-done | bytes 1327136 | tf_op jit(solution)/shard_map/ppermute | solution.py:22
  1056.7 35.1 %collective-permute-done.57 = bf16[288,768]{1,0:T(8,128)(2,1)S(1)} collective-permute-done((bf16[288,768]{1,0:T(8,128)(2,1)S(1)}, bf16[288,768]{1,0:T(8,128)(2,1)S(1)}, u32[]{:S(2)}, u32[]{:S(2)}) %collective-permute-start.57) | collective-permute-done | bytes 442400 | tf_op jit(solution)/shard_map/ppermute | solution.py:22
  1114.8 23.3 %collective-permute-done.55 = bf16[288,768]{1,0:T(8,128)(2,1)} collective-permute-done((bf16[288,768]{1,0:T(8,128)(2,1)}, bf16[288,768]{1,0:T(8,128)(2,1)}, u32[]{:S(2)}, u32[]{:S(2)}) %collective-permute-start.55) | collective-permute-done | bytes 442400 | tf_op jit(solution)/shard_map/ppermute | solution.py:22
  1177.1 19.9 %ladder.9 = (f32[288,1536]{1,0:T(8,128)}, f32[288,1536]{1,0:T(8,128)}) custom-call(s32[4]{0:T(128)} %pad_add_fusion.1.pos_ref, bf16[576,4608]{1,0:T(8,128)(2,1)} %maximum_maximum_fusion.1.lhs_ref, bf16[1152,1536]{1,0:T(8,128)(2,1)} %pad_maximum_fusion.5.v0, bf16[1152,1536]{1,0:T(8,128)(2,1)} %collective-permute-done.9.v1, ...), custom_call_target="tpu_custom_call" | custom-call | flops 10192158720 | bytes 24000000 | tf_op jit(solution)/shard_map/ladder/pallas_call | solution.py:129
  1203.4 20.0 %ladder.10 = (f32[288,1536]{1,0:T(8,128)}, f32[288,1536]{1,0:T(8,128)}) custom-call(s32[4]{0:T(128)} %pad_add_fusion.1.pos_ref, bf16[576,4608]{1,0:T(8,128)(2,1)} %maximum_maximum_fusion.1.lhs_ref, bf16[1152,1536]{1,0:T(8,128)(2,1)} %pad_maximum_fusion.6.v0, bf16[1152,1536]{1,0:T(8,128)(2,1)} %collective-permute-done.29.v1, ...), custom_call_target="tpu_custom_call" | custom-call | flops 10192158720 | bytes 24000000 | tf_op jit(solution)/shard_map/ladder/pallas_call | solution.py:129
  1225.0 19.8 %ladder.11 = (f32[288,1536]{1,0:T(8,128)}, f32[288,1536]{1,0:T(8,128)}) custom-call(s32[4]{0:T(128)} %pad_add_fusion.1.pos_ref, bf16[576,4608]{1,0:T(8,128)(2,1)} %maximum_maximum_fusion.1.lhs_ref, bf16[1152,1536]{1,0:T(8,128)(2,1)} %pad_maximum_fusion.7.v0, bf16[1152,1536]{1,0:T(8,128)(2,1)} %collective-permute-done.45.v1, ...), custom_call_target="tpu_custom_call" | custom-call | flops 10192158720 | bytes 24000000 | tf_op jit(solution)/shard_map/ladder/pallas_call | solution.py:129
  1250.2 27.1 %fold.3.mix_ref = f32[288,4608]{1,0:T(8,128)} custom-call(s32[3]{0:T(128)} %pad_add_fusion.pos_ref, f32[288,2304]{1,0:T(8,128)} %convolution_bitcast_fusion.own_ref, f32[288,2304]{1,0:T(8,128)} %convolution_bitcast_fusion.1.oth_ref, f32[4,288,1152]{2,1,0:T(8,128)} %pad_maximum_fusion.4.s_ref), custom_call_target="tpu_custom_call" | custom-call | flops 20000000000 | bytes 16000000 | tf_op jit(solution)/shard_map/fold/pallas_call | solution.py:87
  1290.8 29.1 %collective-permute-done.79.got_ref = f32[288,1536]{1,0:T(8,128)} collective-permute-done((f32[288,1536]{1,0:T(8,128)}, f32[288,1536]{1,0:T(8,128)}, u32[]{:S(2)}, u32[]{:S(2)}) %collective-permute-start.79) | collective-permute-done | bytes 1769504 | tf_op jit(solution)/shard_map/ppermute | solution.py:18
  (400 shorter events, 537.0 us)
Async XLA Ops:
  0.0 220.2 %collective-permute-start.12 = (bf16[288,4608]{1,0:T(8,128)(2,1)}, bf16[288,4608]{1,0:T(8,128)(2,1)}, u32[]{:S(2)}, u32[]{:S(2)}) collective-permute-start(bf16[288,4608]{1,0:T(8,128)(2,1)} %oovv_ref.11), channel_id=1, source_target_pairs={{0,1},{1,0},{2,3},{3,2},{4,5},{5,4},{6,7},{7,6},{8,9},{9,8},{10,11... | collective-permute-start | bytes 7962632 | tf_op jit(solution)/shard_map/ppermute | solution.py:18
  0.7 165.1 %collective-permute-start.13 = (bf16[288,4608]{1,0:T(8,128)(2,1)}, bf16[288,4608]{1,0:T(8,128)(2,1)}, u32[]{:S(2)}, u32[]{:S(2)}) collective-permute-start(bf16[288,4608]{1,0:T(8,128)(2,1)} %oovv_ref.11), channel_id=1, source_target_pairs={{0,4},{1,5},{2,6},{3,7},{4,0},{5,1},{6,2},{7,3},{8,12},{9,13},{10,... | collective-permute-start | bytes 7962632 | tf_op jit(solution)/shard_map/ppermute | solution.py:18
  15.0 150.9 %collective-permute-start.21 = (bf16[576,2304]{1,0:T(8,128)(2,1)}, bf16[576,2304]{1,0:T(8,128)(2,1)}, u32[]{:S(2)}, u32[]{:S(2)}) collective-permute-start(bf16[576,2304]{1,0:T(8,128)(2,1)} %slice_dynamic-update-slice_fusion.22), channel_id=1, source_target_pairs={{0,8},{8,0},{1,9},{9,1},{2,10},{10,2},{3,11},{11,3},{4,12},{12,4},... | collective-permute-start | bytes 7962632 | tf_op jit(solution)/shard_map/ppermute | solution.py:22
  33.5 126.1 %collective-permute-start = (bf16[288,1536]{1,0:T(8,128)(2,1)}, bf16[288,1536]{1,0:T(8,128)(2,1)}, u32[]{:S(2)}, u32[]{:S(2)}) collective-permute-start(bf16[288,1536]{1,0:T(8,128)(2,1)} %pad_maximum_fusion.10.k0), channel_id=1, source_target_pairs={{0,2},{1,3},{2,0},{3,1},{4,6},{5,7},{6,4},{7,5},{8,10},{9,11},{10,... | collective-permute-start | bytes 2654216 | tf_op jit(solution)/shard_map/ppermute | solution.py:18
  35.9 128.3 %collective-permute-start.1 = (bf16[288,1536]{1,0:T(8,128)(2,1)}, bf16[288,1536]{1,0:T(8,128)(2,1)}, u32[]{:S(2)}, u32[]{:S(2)}) collective-permute-start(bf16[288,1536]{1,0:T(8,128)(2,1)} %pad_maximum_fusion.11.k0), channel_id=1, source_target_pairs={{0,2},{1,3},{2,0},{3,1},{4,6},{5,7},{6,4},{7,5},{8,10},{9,11},{10,... | collective-permute-start | bytes 2654216 | tf_op jit(solution)/shard_map/ppermute | solution.py:18
  165.8 77.9 %collective-permute-start.14 = (bf16[288,4608]{1,0:T(8,128)(2,1)}, bf16[288,4608]{1,0:T(8,128)(2,1)S(1)}, u32[]{:S(2)}, u32[]{:S(2)}) collective-permute-start(bf16[288,4608]{1,0:T(8,128)(2,1)} %collective-permute-done.13), channel_id=1, source_target_pairs={{0,1},{1,0},{2,3},{3,2},{4,5},{5,4},{6,7},{7,6},{8,9},{9,8},{10,11... | collective-permute-start | bytes 7962632 | tf_op jit(solution)/shard_map/ppermute | solution.py:18
  165.9 77.8 %collective-permute-start.23 = (bf16[576,2304]{1,0:T(8,128)(2,1)}, bf16[576,2304]{1,0:T(8,128)(2,1)}, u32[]{:S(2)}, u32[]{:S(2)}) collective-permute-start(bf16[576,2304]{1,0:T(8,128)(2,1)} %collective-permute-done.21), channel_id=1, source_target_pairs={{0,2},{1,3},{2,0},{3,1},{4,6},{5,7},{6,4},{7,5},{8,10},{9,11},{10,... | collective-permute-start | bytes 7962632 | tf_op jit(solution)/shard_map/ppermute | solution.py:18
  218.7 80.0 %collective-permute-start.27 = (bf16[576,2304]{1,0:T(8,128)(2,1)}, bf16[576,2304]{1,0:T(8,128)(2,1)}, u32[]{:S(2)}, u32[]{:S(2)}) collective-permute-start(bf16[576,2304]{1,0:T(8,128)(2,1)} %collective-permute-done.25), channel_id=1, source_target_pairs={{0,2},{1,3},{2,0},{3,1},{4,6},{5,7},{6,4},{7,5},{8,10},{9,11},{10,... | collective-permute-start | bytes 7962632 | tf_op jit(solution)/shard_map/ppermute | solution.py:18
  342.4 91.2 %collective-permute-start.9 = (bf16[1152,1536]{1,0:T(8,128)(2,1)}, bf16[1152,1536]{1,0:T(8,128)(2,1)}, u32[]{:S(2)}, u32[]{:S(2)}) collective-permute-start(bf16[1152,1536]{1,0:T(8,128)(2,1)} %pad_maximum_fusion.5.v0), channel_id=1, source_target_pairs={{0,4},{1,5},{2,6},{3,7},{4,0},{5,1},{6,2},{7,3},{8,12},{9,13},{10,... | collective-permute-start | bytes 10616840 | tf_op jit(solution)/shard_map/ppermute | solution.py:18
  343.3 164.8 %collective-permute-start.29 = (bf16[1152,1536]{1,0:T(8,128)(2,1)}, bf16[1152,1536]{1,0:T(8,128)(2,1)}, u32[]{:S(2)}, u32[]{:S(2)}) collective-permute-start(bf16[1152,1536]{1,0:T(8,128)(2,1)} %pad_maximum_fusion.6.v0), channel_id=1, source_target_pairs={{0,4},{1,5},{2,6},{3,7},{4,0},{5,1},{6,2},{7,3},{8,12},{9,13},{10,... | collective-permute-start | bytes 10616840 | tf_op jit(solution)/shard_map/ppermute | solution.py:18
  359.2 150.4 %collective-permute-start.16 = (bf16[288,1152]{1,0:T(8,128)(2,1)S(1)}, bf16[288,1152]{1,0:T(8,128)(2,1)S(1)}, u32[]{:S(2)}, u32[]{:S(2)}) collective-permute-start(bf16[288,1152]{1,0:T(8,128)(2,1)S(1)} %fusion.17), channel_id=1, source_target_pairs={{0,8},{8,0},{1,9},{9,1},{2,10},{10,2},{3,11},{11,3},{4,12},{12,4},... | collective-permute-start | bytes 1990664 | tf_op jit(solution)/shard_map/ppermute | solution.py:22
  371.0 185.8 %collective-permute-start.10 = (bf16[1152,1536]{1,0:T(8,128)(2,1)}, bf16[1152,1536]{1,0:T(8,128)(2,1)}, u32[]{:S(2)}, u32[]{:S(2)}) collective-permute-start(bf16[1152,1536]{1,0:T(8,128)(2,1)} %pad_maximum_fusion.5.v0), channel_id=1, source_target_pairs={{0,1},{1,0},{2,3},{3,2},{4,5},{5,4},{6,7},{7,6},{8,9},{9,8},{10,11... | collective-permute-start | bytes 10616840 | tf_op jit(solution)/shard_map/ppermute | solution.py:18
  371.0 187.6 %collective-permute-start.30 = (bf16[1152,1536]{1,0:T(8,128)(2,1)}, bf16[1152,1536]{1,0:T(8,128)(2,1)}, u32[]{:S(2)}, u32[]{:S(2)}) collective-permute-start(bf16[1152,1536]{1,0:T(8,128)(2,1)} %pad_maximum_fusion.6.v0), channel_id=1, source_target_pairs={{0,1},{1,0},{2,3},{3,2},{4,5},{5,4},{6,7},{7,6},{8,9},{9,8},{10,11... | collective-permute-start | bytes 10616840 | tf_op jit(solution)/shard_map/ppermute | solution.py:18
  433.5 126.6 %collective-permute-start.11 = (bf16[1152,1536]{1,0:T(8,128)(2,1)}, bf16[1152,1536]{1,0:T(8,128)(2,1)}, u32[]{:S(2)}, u32[]{:S(2)}) collective-permute-start(bf16[1152,1536]{1,0:T(8,128)(2,1)} %collective-permute-done.9.v1), channel_id=1, source_target_pairs={{0,1},{1,0},{2,3},{3,2},{4,5},{5,4},{6,7},{7,6},{8,9},{9,8},{10,11... | collective-permute-start | bytes 10616840 | tf_op jit(solution)/shard_map/ppermute | solution.py:18
  558.5 145.5 %collective-permute-start.45 = (bf16[1152,1536]{1,0:T(8,128)(2,1)S(1)}, bf16[1152,1536]{1,0:T(8,128)(2,1)}, u32[]{:S(2)}, u32[]{:S(2)}) collective-permute-start(bf16[1152,1536]{1,0:T(8,128)(2,1)S(1)} %copy-done.13), channel_id=1, source_target_pairs={{0,4},{1,5},{2,6},{3,7},{4,0},{5,1},{6,2},{7,3},{8,12},{9,13},{10,... | collective-permute-start | bytes 10616840 | tf_op jit(solution)/shard_map/ppermute | solution.py:18
  560.1 132.5 %collective-permute-start.38 = (f32[288,1152]{1,0:T(8,128)}, f32[288,1152]{1,0:T(8,128)}, u32[]{:S(2)}, u32[]{:S(2)}) collective-permute-start(f32[288,1152]{1,0:T(8,128)} %collective-permute-done.37), channel_id=1, source_target_pairs={{0,4},{1,5},{2,6},{3,7},{4,0},{5,1},{6,2},{7,3},{8,12},{9,13},{10,... | collective-permute-start | bytes 3981320 | tf_op jit(solution)/shard_map/ppermute | solution.py:18
  704.1 87.8 %collective-permute-start.46 = (bf16[1152,1536]{1,0:T(8,128)(2,1)S(1)}, bf16[1152,1536]{1,0:T(8,128)(2,1)}, u32[]{:S(2)}, u32[]{:S(2)}) collective-permute-start(bf16[1152,1536]{1,0:T(8,128)(2,1)S(1)} %copy-done.13), channel_id=1, source_target_pairs={{0,1},{1,0},{2,3},{3,2},{4,5},{5,4},{6,7},{7,6},{8,9},{9,8},{10,11... | collective-permute-start | bytes 10616840 | tf_op jit(solution)/shard_map/ppermute | solution.py:18
  704.1 88.7 %collective-permute-start.47 = (bf16[1152,1536]{1,0:T(8,128)(2,1)}, bf16[1152,1536]{1,0:T(8,128)(2,1)}, u32[]{:S(2)}, u32[]{:S(2)}) collective-permute-start(bf16[1152,1536]{1,0:T(8,128)(2,1)} %collective-permute-done.45.v1), channel_id=1, source_target_pairs={{0,1},{1,0},{2,3},{3,2},{4,5},{5,4},{6,7},{7,6},{8,9},{9,8},{10,11... | collective-permute-start | bytes 10616840 | tf_op jit(solution)/shard_map/ppermute | solution.py:18
  706.6 79.4 %collective-permute-start.39 = (f32[288,1152]{1,0:T(8,128)S(1)}, f32[288,1152]{1,0:T(8,128)S(1)}, u32[]{:S(2)}, u32[]{:S(2)}) collective-permute-start(f32[288,1152]{1,0:T(8,128)S(1)} %get-tuple-element.76), channel_id=1, source_target_pairs={{0,1},{1,0},{2,3},{3,2},{4,5},{5,4},{6,7},{7,6},{8,9},{9,8},{10,11... | collective-permute-start | bytes 3981320 | tf_op jit(solution)/shard_map/ppermute | solution.py:18
  787.1 85.7 %collective-permute-start.43 = (f32[288,1536]{1,0:T(8,128)}, f32[288,1536]{1,0:T(8,128)}, u32[]{:S(2)}, u32[]{:S(2)}) collective-permute-start(f32[288,1536]{1,0:T(8,128)} %get-tuple-element.39), channel_id=1, source_target_pairs={{0,2},{1,3},{2,0},{3,1},{4,6},{5,7},{6,4},{7,5},{8,10},{9,11},{10,... | collective-permute-start | bytes 5308424 | tf_op jit(solution)/shard_map/ppermute | solution.py:18
  812.6 130.8 %collective-permute-start.51 = (f32[288,1536]{1,0:T(8,128)}, f32[288,1536]{1,0:T(8,128)S(1)}, u32[]{:S(2)}, u32[]{:S(2)}) collective-permute-start(f32[288,1536]{1,0:T(8,128)} %get-tuple-element.46), channel_id=1, source_target_pairs={{0,2},{1,3},{2,0},{3,1},{4,6},{5,7},{6,4},{7,5},{8,10},{9,11},{10,... | collective-permute-start | bytes 5308424 | tf_op jit(solution)/shard_map/ppermute | solution.py:18
  1014.4 86.3 %collective-permute-start.65 = (f32[288,1152]{1,0:T(8,128)S(1)}, f32[288,1152]{1,0:T(8,128)S(1)}, u32[]{:S(2)}, u32[]{:S(2)}) collective-permute-start(f32[288,1152]{1,0:T(8,128)S(1)} %get-tuple-element.73), channel_id=1, source_target_pairs={{0,8},{8,0},{1,9},{9,1},{2,10},{10,2},{3,11},{11,3},{4,12},{12,4},... | collective-permute-start | bytes 3981320 | tf_op jit(solution)/shard_map/ppermute | solution.py:22
  1016.0 85.2 %collective-permute-start.66 = (f32[288,1152]{1,0:T(8,128)S(1)}, f32[288,1152]{1,0:T(8,128)S(1)}, u32[]{:S(2)}, u32[]{:S(2)}) collective-permute-start(f32[288,1152]{1,0:T(8,128)S(1)} %get-tuple-element.72), channel_id=1, source_target_pairs={{0,4},{1,5},{2,6},{3,7},{4,0},{5,1},{6,2},{7,3},{8,12},{9,13},{10,... | collective-permute-start | bytes 3981320 | tf_op jit(solution)/shard_map/ppermute | solution.py:18
  1025.4 77.4 %collective-permute-start.68 = (f32[288,1152]{1,0:T(8,128)S(1)}, f32[288,1152]{1,0:T(8,128)S(1)}, u32[]{:S(2)}, u32[]{:S(2)}) collective-permute-start(f32[288,1152]{1,0:T(8,128)S(1)} %collective-permute-done.67), channel_id=1, source_target_pairs={{0,4},{1,5},{2,6},{3,7},{4,0},{5,1},{6,2},{7,3},{8,12},{9,13},{10,... | collective-permute-start | bytes 3981320 | tf_op jit(solution)/shard_map/ppermute | solution.py:18
  (119 other events, 3392.7 us)

commit v2 on v1

--- a/solution.py
+++ b/solution.py
@@ -45,6 +45,15 @@
     return jnp.concatenate([p[:, :width] for p in parts] + [p[:, width:] for p in parts], axis=1)
 
 
+def order_kernel(w_ref, perm_ref, out_ref):
+    group = perm_ref.shape[0]
+    half = w_ref.shape[1] // 2
+    for g in range(w_ref.shape[1] // group):
+        moved = jnp.dot(w_ref[:, g * group : (g + 1) * group], perm_ref[...], preferred_element_type=F32).astype(BF16)
+        out_ref[:, g * (group // 2) : (g + 1) * (group // 2)] = moved[:, : group // 2]
+        out_ref[:, half + g * (group // 2) : half + (g + 1) * (group // 2)] = moved[:, group // 2 :]
+
+
 def order_columns(w, n_vir):
     half = n_vir // 2
     group = 8 * n_vir
@@ -52,10 +61,19 @@
     j, rest = src // n_vir, src % n_vir
     dst = (rest // half) * (8 * half) + j * half + rest % half
     perm = (dst[:, None] == jnp.arange(group)[None, :]).astype(BF16)
-    parts = [mm(lax.slice_in_dim(w, g, g + group, axis=1), perm).astype(BF16) for g in range(0, w.shape[1], group)]
-    lo = [p[:, : group // 2] for p in parts]
-    hi = [p[:, group // 2 :] for p in parts]
-    return jnp.concatenate(lo + hi, axis=1)
+    tile = 288
+    block = pl.BlockSpec((tile, w.shape[1]), lambda i: (i, 0))
+    return pl.pallas_call(
+        order_kernel,
+        grid=(w.shape[0] // tile,),
+        out_shape=jax.ShapeDtypeStruct(w.shape, BF16),
+        in_specs=[block, pl.BlockSpec(perm.shape, lambda i: (0, 0))],
+        out_specs=block,
+        cost_estimate=pl.CostEstimate(
+            flops=2 * w.size * group, bytes_accessed=4 * w.size, transcendentals=0
+        ),
+        name="order",
+    )(w, perm)
 
 
 def fold_kernel(occ_l, vir_l, n_occ, n_vir, pos_ref, own_ref, oth_ref, s_ref, out_ref, buf):
@@ -101,8 +119,20 @@
     )(pos, own, oth, s_all)
 
 
-def ladder_kernel(pos_ref, lhs_ref, v0, v1, v2, v3, w_ref, k0, k1, k2, k3, away_ref, home_ref):
+def ladder_kernel(pos_ref, t_ref, *refs):
+    *far, v0, v1, v2, v3, w_ref, k0, k1, k2, k3, away_ref, home_ref, lhs_ref = refs
     depth = v0.shape[0]
+
+    @pl.when(pl.program_id(0) == 0)
+    def _():
+        near = t_ref.shape[1] // 2
+        lhs_ref[:, :near] = t_ref[:, pl.ds(pl.multiple_of(pos_ref[4] * near, 128), near)]
+        rows, wide = far[0].shape
+        count = len(far) // 2
+        for n in range(count):
+            lhs_ref[:rows, near + n * wide : near + (n + 1) * wide] = far[n][...]
+            lhs_ref[rows:, near + n * wide : near + (n + 1) * wide] = far[count + n][...]
+
     acc = None
     for p, v in enumerate((v0, v1, v2, v3)):
         off = pl.multiple_of(pos_ref[p] * depth, 128)
@@ -116,8 +146,8 @@
     home_ref[...] = acc[half:]
 
 
-def ladder(pos, lhs, v, w, k, tile):
-    m, n = lhs.shape[0], v[0].shape[1]
+def ladder(pos, t_rows, far, v, w, k, tile):
+    m, n = t_rows.shape[0], v[0].shape[1]
 
     def full(a):
         return pl.BlockSpec(a.shape, lambda i: (0, 0), pipeline_mode=pl.Buffered(1))
@@ -130,16 +160,18 @@
         ladder_kernel,
         grid=(n // tile,),
         out_shape=(out, out),
-        in_specs=[pl.BlockSpec(memory_space=pltpu.SMEM), full(lhs)]
+        in_specs=[pl.BlockSpec(memory_space=pltpu.SMEM), full(t_rows)]
+        + [full(a) for a in far]
         + [cols(a.shape[0]) for a in v]
         + [full(w)]
         + [cols(a.shape[0]) for a in k],
         out_specs=(cols(m // 2), cols(m // 2)),
+        scratch_shapes=[pltpu.VMEM(t_rows.shape, BF16)],
         cost_estimate=pl.CostEstimate(
-            flops=2 * m * n * (lhs.shape[1] + w.shape[1]), bytes_accessed=24_000_000, transcendentals=0
+            flops=2 * m * n * (t_rows.shape[1] + w.shape[1]), bytes_accessed=24_000_000, transcendentals=0
         ),
         name="ladder",
-    )(pos, lhs, *v, w, *k)
+    )(pos, t_rows, *far, *v, w, *k)
 
 
 def flip_kernel(pos_ref, a0, a1, a2, a3, out_ref, buf):
@@ -211,7 +243,7 @@
     def local_sweeps(t_block, d_block, oovv_block, vvvv_block, oooo_full, w_block):
         n_occ = math.isqrt(oooo_full.shape[0])
         n_vir = w_block.shape[0] // n_occ
-        rows, cols = t_block.shape
+        rows, _ = t_block.shape
         occ_l = n_occ // 8
         vir_l = n_vir // 2
         row = lax.axis_index("row")
@@ -219,7 +251,7 @@
         y, x, c = row // 4, (row // 2) % 2, row % 2
         y_is_z = y == z
         pos_fold = jnp.stack([x, c, z]).astype(jnp.int32)
-        pos_ladder = jnp.stack([((y ^ dy) ^ z) * 2 + (c ^ dc) for dy, dc in ((0, 0), (1, 0), (0, 1), (1, 1))])
+        pos_ladder = jnp.stack([((y ^ dy) ^ z) * 2 + (c ^ dc) for dy, dc in ((0, 0), (1, 0), (0, 1), (1, 1))] + [x])
         pos_ladder = pos_ladder.astype(jnp.int32)
 
         pos_flip = jnp.stack([2 * (y ^ dy) + (z ^ dz) for dy, dz in ((0, 0), (0, 1), (1, 0), (1, 1))])
@@ -232,14 +264,16 @@
             for s in range(2)
         ]
         t_first = split_cols(after(t_block, *w_sends).astype(BF16), N_CHUNK)
-        w_oth = jnp.zeros(w_block.shape, BF16)
+        w_list, w_starts = [], []
         for s in range(2):
             w_got = swap_col(w_sends[s])
             w_far = swap_row(w_got, X_BIT)
             w_q = [w_got, swap_row(w_got, CORE_BIT), w_far, swap_row(w_far, CORE_BIT)]
             for m in range(4):
-                start = ((2 * x + c) ^ m) * quarter + s * piece
-                w_oth = lax.dynamic_update_slice_in_dim(w_oth, w_q[m], start, axis=0)
+                w_starts.append((((2 * x + c) ^ m) * quarter + s * piece) // n_vir)
+                w_list.append(w_q[m])
+        w_oth = jnp.concatenate(w_list, axis=0)
+        n_list = piece // n_vir
         w_own = order_columns(after(w_block, *t_first), n_vir)
         w_own = w_own.reshape(n_occ, n_vir, w_own.shape[1])
         w_oth = w_oth.reshape(n_occ, n_vir, w_oth.shape[1])
@@ -271,7 +305,7 @@
             tx_full = join_cols(t_x)
 
             def far(send):
-                return jnp.concatenate([swap_col(p) for p in send], axis=1)
+                return [swap_col(p) for p in send]
 
             t_rows = jnp.concatenate([tx_full, t_full], axis=0)
             if not last:
@@ -279,11 +313,12 @@
                     fetch_v(n, v_near[n])
 
             t_four = t_full.reshape(occ_l, n_occ, vir_l, n_vir)
+            t_oth = jnp.concatenate([lax.dynamic_slice_in_dim(t_four, k, n_list, axis=1) for k in w_starts], axis=1)
             mix_own = mixed_product(t_four, w_own)
             far_own = far(near_parts)
 
             if last:
-                mix_oth = mixed_product(t_four, w_oth)
+                mix_oth = mixed_product(t_oth, w_oth)
                 t_rows = after(t_rows, mix_oth)
             inter = mm(t_rows, oovv_set, (((1,), (1,)), ((), ())))
             inter_send = cut(inter, 1 - z, rows, 0)
@@ -295,11 +330,9 @@
             near_x = [near_half(p) for p in t_x[:-1]]
             near_x.append(near_half(after(t_x[-1], *near_x)))
             far_x = far(near_x)
-            near = cut(t_rows, x, cols // 2, 1)
-            lhs = jnp.concatenate([near, jnp.concatenate([far_x, far_own], axis=0)], axis=1)
 
             if not last:
-                t_late = after(t_four, hole_half)
+                t_late = after(t_oth, hole_half)
                 mix_oth = mixed_product(t_late, w_oth)
 
             half_w = mix_own.shape[1] // 2
@@ -311,7 +344,7 @@
 
             def ladder_part(n):
                 k_rows = (t_parts[n], t_c[n], t_y[n], t_yc[n])
-                away, home = ladder(pos_ladder, lhs, v_set[n], hole_w, k_rows, 512)
+                away, home = ladder(pos_ladder, t_rows, far_x + far_own, v_set[n], hole_w, k_rows, 256)
                 return away, home, swap_row(away, X_BIT)
 
             here = pick(y_is_z, keep_own, keep_oth)

time: 1340 us -> 1230 us (0.918)
  waiting for transfers between devices: 701 us -> 642 us
  Pallas kernels: 214 us -> 256 us
  matrix products: 104 us -> 69.5 us
  other arithmetic: 80 us -> 50.3 us
  local copies, waits for them, and re-layouts: 167 us -> 144 us
    ppermute x58, waiting for transfers between devices: 533 us -> 473 us  [swap_row(): return lax.ppermute(value, 'row', [(i, i ^ bit) for i in range(8)])]
    dot_general x11 -> x2, matrix products: 59.7 us -> 20.8 us  [mm(): return lax.dot_general(lhs, rhs, dims, preferred_element_type=F32)]
    pallas_call x0 -> x3, Pallas kernels: none -> 37.4 us  [order_columns(): pl.pallas_call(order_kernel, grid=(w.shape[0] // tile,), out_shape=jax.Sh...]
    concatenate x2 -> x0, other arithmetic: 28.8 us -> none  [sweep(): jnp.concatenate([near, jnp.concatenate([far_x, far_own], axis=0)], axis=1)]
    concatenate x4 -> x3, local copies, waits for them, and re-layouts: 30.4 us -> 3.6 us  [the longest x2 1.95 us: sweep(): jnp.concatenate([lax.dynamic_slice_in_dim(t_four, k, n_list, axis=1) for...]
    unnamed x164 -> x180, local copies, waits for them, and re-layouts: 62.1 us -> 71.8 us
  transfers between devices with their start and end apart: 80 -> 80, of which waited for: 27 -> 28; matrix products, arithmetic and copies ran while one was open for 25% -> 21% of each run, Pallas kernels for 15% -> 20%
where the time goes in v2:
time: 1230 us; the launch traced here: 1210 us
  waiting for transfers between devices  642 us (52%)
  Pallas kernels  256 us (21%)
  local copies, waits for them, and re-layouts  144 us (12%)
  matrix products  69.5 us (6%)
  starting transfers between devices  51.3 us (4%)
  other arithmetic  50.3 us (4%)
    ppermute x58, waiting for transfers between devices, swap_row(): return lax.ppermute(value, 'row', [(i, i ^ bit) for i in range(8)])  473 us
    ppermute x22, waiting for transfers between devices, swap_col(): return lax.ppermute(value, 'col', [(0, 1), (1, 0)])  169 us
    pallas_call x6, Pallas kernels, ladder(): pl.pallas_call(ladder_kernel, grid=(n // tile,), out_shape=(out, out), in...  123 us
    unnamed x180, local copies, waits for them, and re-layouts  71.8 us
    pallas_call x2, Pallas kernels, fold(): pl.pallas_call(functools.partial(fold_kernel, occ_l, vir_l, n_occ, n_vir)...  54.2 us
    dot_general x4, matrix products, mixed_product(): out = jnp.einsum('ikac,kcn->ian', t_four, w, preferred_element_type=F32)  48.7 us
    pallas_call x3, Pallas kernels, order_columns(): pl.pallas_call(order_kernel, grid=(w.shape[0] // tile,), out_shape=jax.Sh...  37.4 us
    ppermute x58, starting transfers between devices, swap_row(): return lax.ppermute(value, 'row', [(i, i ^ bit) for i in range(8)])  33.6 us
  transfers between devices with their start and end apart: 80, of which 28 were waited for; matrix products, arithmetic and copies ran while one was open for 21% of the time, Pallas kernels for 20%

profile of v2, /device:TPU:0, one launch (start us, length us, event | category | flops | bytes accessed | tf_op | source)
XLA Modules:
  0.0 1214.1 jit_solution(6121562385410688032)
XLA Ops:
  45.9 27.0 %order.5 = bf16[4608,2304]{1,0:T(8,128)(2,1)} custom-call(bf16[4608,2304]{1,0:T(8,128)(2,1)} %w_ref, bf16[768,768]{1,0:T(8,128)(2,1)} %fusion.perm_ref), custom_call_target="tpu_custom_call" | custom-call | flops 16307453952 | bytes 42467328 | tf_op jit(solution)/shard_map/order/pallas_call | solution.py:66
  159.7 28.8 %collective-permute-done.25 = bf16[576,2304]{1,0:T(8,128)(2,1)S(1)} collective-permute-done((bf16[576,2304]{1,0:T(8,128)(2,1)S(1)}, bf16[576,2304]{1,0:T(8,128)(2,1)S(1)}, u32[]{:S(2)}, u32[]{:S(2)}) %collective-permute-start.25) | collective-permute-done | bytes 2654240 | tf_op jit(solution)/shard_map/ppermute | solution.py:22
  235.8 23.7 %collective-permute-done.27 = bf16[576,2304]{1,0:T(8,128)(2,1)S(1)} collective-permute-done((bf16[576,2304]{1,0:T(8,128)(2,1)S(1)}, bf16[576,2304]{1,0:T(8,128)(2,1)S(1)}, u32[]{:S(2)}, u32[]{:S(2)}) %collective-permute-start.27) | collective-permute-done | bytes 2654240 | tf_op jit(solution)/shard_map/ppermute | solution.py:18
  275.1 55.0 %collective-permute-done.18.refs_13_ = bf16[288,1536]{1,0:T(8,128)(2,1)S(1)} collective-permute-done((bf16[288,1536]{1,0:T(8,128)(2,1)}, bf16[288,1536]{1,0:T(8,128)(2,1)S(1)}, u32[]{:S(2)}, u32[]{:S(2)}) %collective-permute-start.18) | collective-permute-done | bytes 884768 | tf_op jit(solution)/shard_map/ppermute | solution.py:18
  373.3 53.3 %collective-permute-done.29.refs_7_ = bf16[1152,1536]{1,0:T(8,128)(2,1)} collective-permute-done((bf16[1152,1536]{1,0:T(8,128)(2,1)}, bf16[1152,1536]{1,0:T(8,128)(2,1)}, u32[]{:S(2)}, u32[]{:S(2)}) %collective-permute-start.29) | collective-permute-done | bytes 3538976 | tf_op jit(solution)/shard_map/ppermute | solution.py:18
  433.6 24.0 %collective-permute-done.37 = f32[288,1152]{1,0:T(8,128)} collective-permute-done((f32[288,1152]{1,0:T(8,128)}, f32[288,1152]{1,0:T(8,128)}, u32[]{:S(2)}, u32[]{:S(2)}) %collective-permute-start.37) | collective-permute-done | bytes 1327136 | tf_op jit(solution)/shard_map/ppermute | solution.py:22
  465.1 20.6 %ladder.6 = (f32[288,1536]{1,0:T(8,128)}, f32[288,1536]{1,0:T(8,128)}) custom-call(s32[5]{0:T(128)} %stack.81.pos_ref, bf16[576,4608]{1,0:T(8,128)(2,1)} %pad_maximum_fusion.t_ref, bf16[288,768]{1,0:T(8,128)(2,1)} %copy-done.58, bf16[288,768]{1,0:T(8,128)(2,1)} %copy-done.59, bf16[288,768]{1,0:T(8,128)(2,1)} %copy-done.60, bf16[288,768]{1,0:T(8,128)(2,1)} %copy-done.55, ...), custom_call_target="tpu_custom_call" | custom-call | flops 10192158720 | bytes 24000000 | tf_op jit(solution)/shard_map/ladder/pallas_call | solution.py:159
  485.7 20.6 %ladder.7 = (f32[288,1536]{1,0:T(8,128)}, f32[288,1536]{1,0:T(8,128)}) custom-call(s32[5]{0:T(128)} %stack.81.pos_ref, bf16[576,4608]{1,0:T(8,128)(2,1)} %pad_maximum_fusion.t_ref, bf16[288,768]{1,0:T(8,128)(2,1)} %copy-done.58, bf16[288,768]{1,0:T(8,128)(2,1)} %copy-done.59, bf16[288,768]{1,0:T(8,128)(2,1)} %copy-done.60, bf16[288,768]{1,0:T(8,128)(2,1)} %copy-done.55, ...), custom_call_target="tpu_custom_call" | custom-call | flops 10192158720 | bytes 24000000 | tf_op jit(solution)/shard_map/ladder/pallas_call | solution.py:159
  506.3 91.6 %collective-permute-done.38.a3 = f32[288,1152]{1,0:T(8,128)} collective-permute-done((f32[288,1152]{1,0:T(8,128)}, f32[288,1152]{1,0:T(8,128)}, u32[]{:S(2)}, u32[]{:S(2)}) %collective-permute-start.38) | collective-permute-done | bytes 1327136 | tf_op jit(solution)/shard_map/ppermute | solution.py:18
  612.0 55.3 %collective-permute-done.40 = f32[576,1152]{1,0:T(8,128)S(1)} collective-permute-done((f32[576,1152]{1,0:T(8,128)}, f32[576,1152]{1,0:T(8,128)S(1)}, u32[]{:S(2)}, u32[]{:S(2)}) %collective-permute-start.40) | collective-permute-done | bytes 2654240 | tf_op jit(solution)/shard_map/ppermute | solution.py:18
  668.1 21.5 %collective-permute-done.49.refs_13_ = bf16[288,1536]{1,0:T(8,128)(2,1)S(1)} collective-permute-done((bf16[288,1536]{1,0:T(8,128)(2,1)S(1)}, bf16[288,1536]{1,0:T(8,128)(2,1)S(1)}, u32[]{:S(2)}, u32[]{:S(2)}) %collective-permute-start.49) | collective-permute-done | bytes 884768 | tf_op jit(solution)/shard_map/ppermute | solution.py:18
  696.8 20.5 %ladder.8 = (f32[288,1536]{1,0:T(8,128)}, f32[288,1536]{1,0:T(8,128)}) custom-call(s32[5]{0:T(128)} %stack.81.pos_ref, bf16[576,4608]{1,0:T(8,128)(2,1)} %pad_maximum_fusion.t_ref, bf16[288,768]{1,0:T(8,128)(2,1)} %copy-done.58, bf16[288,768]{1,0:T(8,128)(2,1)} %copy-done.59, bf16[288,768]{1,0:T(8,128)(2,1)} %copy-done.60, bf16[288,768]{1,0:T(8,128)(2,1)} %copy-done.55, ...), custom_call_target="tpu_custom_call" | custom-call | flops 10192158720 | bytes 24000000 | tf_op jit(solution)/shard_map/ladder/pallas_call | solution.py:159
  718.5 27.1 %fold.2.mix_ref = f32[288,4608]{1,0:T(8,128)} custom-call(s32[3]{0:T(128)} %pad_add_fusion.pos_ref, f32[288,2304]{1,0:T(8,128)} %convolution_bitcast_fusion.3.own_ref, f32[288,2304]{1,0:T(8,128)} %copy-done.18, f32[4,288,1152]{2,1,0:T(8,128)} %pad_maximum_fusion.1.s_ref), custom_call_target="tpu_custom_call" | custom-call | flops 20000000000 | bytes 16000000 | tf_op jit(solution)/shard_map/fold/pallas_call | solution.py:105
  752.3 18.1 %collective-permute-done.43.got_ref = f32[288,1536]{1,0:T(8,128)S(1)} collective-permute-done((f32[288,1536]{1,0:T(8,128)}, f32[288,1536]{1,0:T(8,128)S(1)}, u32[]{:S(2)}, u32[]{:S(2)}) %collective-permute-start.43) | collective-permute-done | bytes 1769504 | tf_op jit(solution)/shard_map/ppermute | solution.py:18
  781.2 46.0 %collective-permute-done.42 = bf16[288,1536]{1,0:T(8,128)(2,1)S(1)} collective-permute-done((bf16[288,1536]{1,0:T(8,128)(2,1)}, bf16[288,1536]{1,0:T(8,128)(2,1)S(1)}, u32[]{:S(2)}, u32[]{:S(2)}) %collective-permute-start.42) | collective-permute-done | bytes 884768 | tf_op jit(solution)/shard_map/ppermute | solution.py:18
  828.1 17.1 %collective-permute-done.44 = bf16[288,1536]{1,0:T(8,128)(2,1)S(1)} collective-permute-done((bf16[288,1536]{1,0:T(8,128)(2,1)}, bf16[288,1536]{1,0:T(8,128)(2,1)S(1)}, u32[]{:S(2)}, u32[]{:S(2)}) %collective-permute-start.44) | collective-permute-done | bytes 884768 | tf_op jit(solution)/shard_map/ppermute | solution.py:18
  903.6 47.1 %collective-permute-done.67 = f32[288,1152]{1,0:T(8,128)S(1)} collective-permute-done((f32[288,1152]{1,0:T(8,128)S(1)}, f32[288,1152]{1,0:T(8,128)S(1)}, u32[]{:S(2)}, u32[]{:S(2)}) %collective-permute-start.67) | collective-permute-done | bytes 1327136 | tf_op jit(solution)/shard_map/ppermute | solution.py:22
  965.3 17.4 %collective-permute-done.68.a3 = f32[288,1152]{1,0:T(8,128)S(1)} collective-permute-done((f32[288,1152]{1,0:T(8,128)S(1)}, f32[288,1152]{1,0:T(8,128)S(1)}, u32[]{:S(2)}, u32[]{:S(2)}) %collective-permute-start.68) | collective-permute-done | bytes 1327136 | tf_op jit(solution)/shard_map/ppermute | solution.py:18
  1020.0 18.6 %collective-permute-done.58.refs_5_ = bf16[288,768]{1,0:T(8,128)(2,1)S(1)} collective-permute-done((bf16[288,768]{1,0:T(8,128)(2,1)S(1)}, bf16[288,768]{1,0:T(8,128)(2,1)S(1)}, u32[]{:S(2)}, u32[]{:S(2)}) %collective-permute-start.58) | collective-permute-done | bytes 442400 | tf_op jit(solution)/shard_map/ppermute | solution.py:22
  1063.0 20.7 %ladder.9 = (f32[288,1536]{1,0:T(8,128)}, f32[288,1536]{1,0:T(8,128)}) custom-call(s32[5]{0:T(128)} %stack.81.pos_ref, bf16[576,4608]{1,0:T(8,128)(2,1)} %copy-done.9, bf16[288,768]{1,0:T(8,128)(2,1)} %copy-done.65, bf16[288,768]{1,0:T(8,128)(2,1)} %copy-done.66, bf16[288,768]{1,0:T(8,128)(2,1)} %copy-done.67, ...), custom_call_target="tpu_custom_call" | custom-call | flops 10192158720 | bytes 24000000 | tf_op jit(solution)/shard_map/ladder/pallas_call | solution.py:159
  1087.7 20.6 %ladder.10 = (f32[288,1536]{1,0:T(8,128)}, f32[288,1536]{1,0:T(8,128)}) custom-call(s32[5]{0:T(128)} %stack.81.pos_ref, bf16[576,4608]{1,0:T(8,128)(2,1)} %copy-done.9, bf16[288,768]{1,0:T(8,128)(2,1)} %copy-done.65, bf16[288,768]{1,0:T(8,128)(2,1)} %copy-done.66, bf16[288,768]{1,0:T(8,128)(2,1)} %copy-done.67, ...), custom_call_target="tpu_custom_call" | custom-call | flops 10192158720 | bytes 24000000 | tf_op jit(solution)/shard_map/ladder/pallas_call | solution.py:159
  1109.9 20.5 %ladder.11 = (f32[288,1536]{1,0:T(8,128)}, f32[288,1536]{1,0:T(8,128)}) custom-call(s32[5]{0:T(128)} %stack.81.pos_ref, bf16[576,4608]{1,0:T(8,128)(2,1)} %copy-done.9, bf16[288,768]{1,0:T(8,128)(2,1)} %copy-done.65, bf16[288,768]{1,0:T(8,128)(2,1)} %copy-done.66, bf16[288,768]{1,0:T(8,128)(2,1)} %copy-done.67, ...), custom_call_target="tpu_custom_call" | custom-call | flops 10192158720 | bytes 24000000 | tf_op jit(solution)/shard_map/ladder/pallas_call | solution.py:159
  1135.4 27.1 %fold.3.mix_ref = f32[288,4608]{1,0:T(8,128)} custom-call(s32[3]{0:T(128)} %pad_add_fusion.pos_ref, f32[288,2304]{1,0:T(8,128)} %copy-done.17, f32[288,2304]{1,0:T(8,128)} %copy-done.16, f32[4,288,1152]{2,1,0:T(8,128)} %pad_maximum_fusion.3.s_ref), custom_call_target="tpu_custom_call" | custom-call | flops 20000000000 | bytes 16000000 | tf_op jit(solution)/shard_map/fold/pallas_call | solution.py:105
  1175.9 28.0 %collective-permute-done.79.got_ref = f32[288,1536]{1,0:T(8,128)} collective-permute-done((f32[288,1536]{1,0:T(8,128)}, f32[288,1536]{1,0:T(8,128)}, u32[]{:S(2)}, u32[]{:S(2)}) %collective-permute-start.79) | collective-permute-done | bytes 1769504 | tf_op jit(solution)/shard_map/ppermute | solution.py:18
  (398 shorter events, 463.1 us)
Async XLA Ops:
  0.0 151.2 %collective-permute-start.12 = (bf16[288,4608]{1,0:T(8,128)(2,1)}, bf16[288,4608]{1,0:T(8,128)(2,1)}, u32[]{:S(2)}, u32[]{:S(2)}) collective-permute-start(bf16[288,4608]{1,0:T(8,128)(2,1)} %oovv_ref.11), channel_id=1, source_target_pairs={{0,1},{1,0},{2,3},{3,2},{4,5},{5,4},{6,7},{7,6},{8,9},{9,8},{10,11... | collective-permute-start | bytes 7962632 | tf_op jit(solution)/shard_map/ppermute | solution.py:18
  0.7 127.8 %collective-permute-start.13 = (bf16[288,4608]{1,0:T(8,128)(2,1)}, bf16[288,4608]{1,0:T(8,128)(2,1)}, u32[]{:S(2)}, u32[]{:S(2)}) collective-permute-start(bf16[288,4608]{1,0:T(8,128)(2,1)} %oovv_ref.11), channel_id=1, source_target_pairs={{0,4},{1,5},{2,6},{3,7},{4,0},{5,1},{6,2},{7,3},{8,12},{9,13},{10,... | collective-permute-start | bytes 7962632 | tf_op jit(solution)/shard_map/ppermute | solution.py:18
  15.0 113.5 %collective-permute-start.21 = (bf16[576,2304]{1,0:T(8,128)(2,1)}, bf16[576,2304]{1,0:T(8,128)(2,1)}, u32[]{:S(2)}, u32[]{:S(2)}) collective-permute-start(bf16[576,2304]{1,0:T(8,128)(2,1)} %order.3), channel_id=1, source_target_pairs={{0,8},{8,0},{1,9},{9,1},{2,10},{10,2},{3,11},{11,3},{4,12},{12,4},... | collective-permute-start | bytes 7962632 | tf_op jit(solution)/shard_map/ppermute | solution.py:22
  27.0 97.8 %collective-permute-start.1 = (bf16[288,1536]{1,0:T(8,128)(2,1)}, bf16[288,1536]{1,0:T(8,128)(2,1)}, u32[]{:S(2)}, u32[]{:S(2)}) collective-permute-start(bf16[288,1536]{1,0:T(8,128)(2,1)} %pad_maximum_fusion.10.refs_11_), channel_id=1, source_target_pairs={{0,2},{1,3},{2,0},{3,1},{4,6},{5,7},{6,4},{7,5},{8,10},{9,11},{10,... | collective-permute-start | bytes 2654216 | tf_op jit(solution)/shard_map/ppermute | solution.py:18
  29.5 98.6 %collective-permute-start = (bf16[288,1536]{1,0:T(8,128)(2,1)}, bf16[288,1536]{1,0:T(8,128)(2,1)}, u32[]{:S(2)}, u32[]{:S(2)}) collective-permute-start(bf16[288,1536]{1,0:T(8,128)(2,1)} %pad_maximum_fusion.9.refs_11_), channel_id=1, source_target_pairs={{0,2},{1,3},{2,0},{3,1},{4,6},{5,7},{6,4},{7,5},{8,10},{9,11},{10,... | collective-permute-start | bytes 2654216 | tf_op jit(solution)/shard_map/ppermute | solution.py:18
  128.5 75.7 %collective-permute-start.23 = (bf16[576,2304]{1,0:T(8,128)(2,1)}, bf16[576,2304]{1,0:T(8,128)(2,1)S(1)}, u32[]{:S(2)}, u32[]{:S(2)}) collective-permute-start(bf16[576,2304]{1,0:T(8,128)(2,1)} %collective-permute-done.21), channel_id=1, source_target_pairs={{0,2},{1,3},{2,0},{3,1},{4,6},{5,7},{6,4},{7,5},{8,10},{9,11},{10,... | collective-permute-start | bytes 7962632 | tf_op jit(solution)/shard_map/ppermute | solution.py:18
  231.6 126.2 %collective-permute-start.9 = (bf16[1152,1536]{1,0:T(8,128)(2,1)}, bf16[1152,1536]{1,0:T(8,128)(2,1)}, u32[]{:S(2)}, u32[]{:S(2)}) collective-permute-start(bf16[1152,1536]{1,0:T(8,128)(2,1)} %pad_maximum_fusion.4.refs_6_), channel_id=1, source_target_pairs={{0,4},{1,5},{2,6},{3,7},{4,0},{5,1},{6,2},{7,3},{8,12},{9,13},{10,... | collective-permute-start | bytes 10616840 | tf_op jit(solution)/shard_map/ppermute | solution.py:18
  259.5 72.6 %collective-permute-start.28 = (bf16[576,2304]{1,0:T(8,128)(2,1)S(1)}, bf16[576,2304]{1,0:T(8,128)(2,1)S(1)}, u32[]{:S(2)}, u32[]{:S(2)}) collective-permute-start(bf16[576,2304]{1,0:T(8,128)(2,1)S(1)} %collective-permute-done.27), channel_id=1, source_target_pairs={{0,1},{1,0},{2,3},{3,2},{4,5},{5,4},{6,7},{7,6},{8,9},{9,8},{10,11... | collective-permute-start | bytes 7962632 | tf_op jit(solution)/shard_map/ppermute | solution.py:18
  272.0 75.3 %collective-permute-start.33 = (bf16[288,1536]{1,0:T(8,128)(2,1)}, bf16[288,1536]{1,0:T(8,128)(2,1)S(1)}, u32[]{:S(2)}, u32[]{:S(2)}) collective-permute-start(bf16[288,1536]{1,0:T(8,128)(2,1)} %pad_maximum_fusion.10.refs_11_), channel_id=1, source_target_pairs={{0,4},{1,5},{2,6},{3,7},{4,0},{5,1},{6,2},{7,3},{8,12},{9,13},{10,... | collective-permute-start | bytes 2654216 | tf_op jit(solution)/shard_map/ppermute | solution.py:18
  347.3 115.2 %collective-permute-start.10 = (bf16[1152,1536]{1,0:T(8,128)(2,1)}, bf16[1152,1536]{1,0:T(8,128)(2,1)}, u32[]{:S(2)}, u32[]{:S(2)}) collective-permute-start(bf16[1152,1536]{1,0:T(8,128)(2,1)} %pad_maximum_fusion.4.refs_6_), channel_id=1, source_target_pairs={{0,1},{1,0},{2,3},{3,2},{4,5},{5,4},{6,7},{7,6},{8,9},{9,8},{10,11... | collective-permute-start | bytes 10616840 | tf_op jit(solution)/shard_map/ppermute | solution.py:18
  347.4 79.2 %collective-permute-start.29 = (bf16[1152,1536]{1,0:T(8,128)(2,1)}, bf16[1152,1536]{1,0:T(8,128)(2,1)}, u32[]{:S(2)}, u32[]{:S(2)}) collective-permute-start(bf16[1152,1536]{1,0:T(8,128)(2,1)} %pad_maximum_fusion.5.refs_6_), channel_id=1, source_target_pairs={{0,4},{1,5},{2,6},{3,7},{4,0},{5,1},{6,2},{7,3},{8,12},{9,13},{10,... | collective-permute-start | bytes 10616840 | tf_op jit(solution)/shard_map/ppermute | solution.py:18
  352.7 110.4 %collective-permute-start.30 = (bf16[1152,1536]{1,0:T(8,128)(2,1)}, bf16[1152,1536]{1,0:T(8,128)(2,1)}, u32[]{:S(2)}, u32[]{:S(2)}) collective-permute-start(bf16[1152,1536]{1,0:T(8,128)(2,1)} %pad_maximum_fusion.5.refs_6_), channel_id=1, source_target_pairs={{0,1},{1,0},{2,3},{3,2},{4,5},{5,4},{6,7},{7,6},{8,9},{9,8},{10,11... | collective-permute-start | bytes 10616840 | tf_op jit(solution)/shard_map/ppermute | solution.py:18
  357.8 106.7 %collective-permute-start.11 = (bf16[1152,1536]{1,0:T(8,128)(2,1)}, bf16[1152,1536]{1,0:T(8,128)(2,1)}, u32[]{:S(2)}, u32[]{:S(2)}) collective-permute-start(bf16[1152,1536]{1,0:T(8,128)(2,1)} %collective-permute-done.9.refs_7_), channel_id=1, source_target_pairs={{0,1},{1,0},{2,3},{3,2},{4,5},{5,4},{6,7},{7,6},{8,9},{9,8},{10,11... | collective-permute-start | bytes 10616840 | tf_op jit(solution)/shard_map/ppermute | solution.py:18
  463.1 146.4 %collective-permute-start.45 = (bf16[1152,1536]{1,0:T(8,128)(2,1)}, bf16[1152,1536]{1,0:T(8,128)(2,1)}, u32[]{:S(2)}, u32[]{:S(2)}) collective-permute-start(bf16[1152,1536]{1,0:T(8,128)(2,1)} %pad_maximum_fusion.6.refs_6_), channel_id=1, source_target_pairs={{0,4},{1,5},{2,6},{3,7},{4,0},{5,1},{6,2},{7,3},{8,12},{9,13},{10,... | collective-permute-start | bytes 10616840 | tf_op jit(solution)/shard_map/ppermute | solution.py:18
  464.5 133.4 %collective-permute-start.38 = (f32[288,1152]{1,0:T(8,128)}, f32[288,1152]{1,0:T(8,128)}, u32[]{:S(2)}, u32[]{:S(2)}) collective-permute-start(f32[288,1152]{1,0:T(8,128)} %collective-permute-done.37), channel_id=1, source_target_pairs={{0,4},{1,5},{2,6},{3,7},{4,0},{5,1},{6,2},{7,3},{8,12},{9,13},{10,... | collective-permute-start | bytes 3981320 | tf_op jit(solution)/shard_map/ppermute | solution.py:18
  609.5 86.4 %collective-permute-start.46 = (bf16[1152,1536]{1,0:T(8,128)(2,1)}, bf16[1152,1536]{1,0:T(8,128)(2,1)}, u32[]{:S(2)}, u32[]{:S(2)}) collective-permute-start(bf16[1152,1536]{1,0:T(8,128)(2,1)} %pad_maximum_fusion.6.refs_6_), channel_id=1, source_target_pairs={{0,1},{1,0},{2,3},{3,2},{4,5},{5,4},{6,7},{7,6},{8,9},{9,8},{10,11... | collective-permute-start | bytes 10616840 | tf_op jit(solution)/shard_map/ppermute | solution.py:18
  609.5 87.4 %collective-permute-start.47 = (bf16[1152,1536]{1,0:T(8,128)(2,1)}, bf16[1152,1536]{1,0:T(8,128)(2,1)}, u32[]{:S(2)}, u32[]{:S(2)}) collective-permute-start(bf16[1152,1536]{1,0:T(8,128)(2,1)} %collective-permute-done.45.refs_7_), channel_id=1, source_target_pairs={{0,1},{1,0},{2,3},{3,2},{4,5},{5,4},{6,7},{7,6},{8,9},{9,8},{10,11... | collective-permute-start | bytes 10616840 | tf_op jit(solution)/shard_map/ppermute | solution.py:18
  612.0 77.6 %collective-permute-start.39 = (f32[288,1152]{1,0:T(8,128)S(1)}, f32[288,1152]{1,0:T(8,128)S(1)}, u32[]{:S(2)}, u32[]{:S(2)}) collective-permute-start(f32[288,1152]{1,0:T(8,128)S(1)} %get-tuple-element.78), channel_id=1, source_target_pairs={{0,1},{1,0},{2,3},{3,2},{4,5},{5,4},{6,7},{7,6},{8,9},{9,8},{10,11... | collective-permute-start | bytes 3981320 | tf_op jit(solution)/shard_map/ppermute | solution.py:18
  694.9 75.4 %collective-permute-start.43 = (f32[288,1536]{1,0:T(8,128)}, f32[288,1536]{1,0:T(8,128)S(1)}, u32[]{:S(2)}, u32[]{:S(2)}) collective-permute-start(f32[288,1536]{1,0:T(8,128)} %get-tuple-element.39), channel_id=1, source_target_pairs={{0,2},{1,3},{2,0},{3,1},{4,6},{5,7},{6,4},{7,5},{8,10},{9,11},{10,... | collective-permute-start | bytes 5308424 | tf_op jit(solution)/shard_map/ppermute | solution.py:18
  717.3 129.7 %collective-permute-start.51 = (f32[288,1536]{1,0:T(8,128)}, f32[288,1536]{1,0:T(8,128)}, u32[]{:S(2)}, u32[]{:S(2)}) collective-permute-start(f32[288,1536]{1,0:T(8,128)} %get-tuple-element.46), channel_id=1, source_target_pairs={{0,2},{1,3},{2,0},{3,1},{4,6},{5,7},{6,4},{7,5},{8,10},{9,11},{10,... | collective-permute-start | bytes 5308424 | tf_op jit(solution)/shard_map/ppermute | solution.py:18
  751.3 75.9 %collective-permute-start.42 = (bf16[288,1536]{1,0:T(8,128)(2,1)}, bf16[288,1536]{1,0:T(8,128)(2,1)S(1)}, u32[]{:S(2)}, u32[]{:S(2)}) collective-permute-start(bf16[288,1536]{1,0:T(8,128)(2,1)} %get-tuple-element.41.refs_11_), channel_id=1, source_target_pairs={{0,2},{1,3},{2,0},{3,1},{4,6},{5,7},{6,4},{7,5},{8,10},{9,11},{10,... | collective-permute-start | bytes 2654216 | tf_op jit(solution)/shard_map/ppermute | solution.py:18
  1001.7 82.0 %collective-permute-start.70 = (f32[576,1152]{1,0:T(8,128)}, f32[576,1152]{1,0:T(8,128)}, u32[]{:S(2)}, u32[]{:S(2)}) collective-permute-start(f32[576,1152]{1,0:T(8,128)} %constant_dynamic-slice_fusion.1), channel_id=1, source_target_pairs={{0,2},{1,3},{2,0},{3,1},{4,6},{5,7},{6,4},{7,5},{8,10},{9,11},{10,... | collective-permute-start | bytes 7962632 | tf_op jit(solution)/shard_map/ppermute | solution.py:18
  1087.2 75.2 %collective-permute-start.64 = (f32[288,1536]{1,0:T(8,128)}, f32[288,1536]{1,0:T(8,128)}, u32[]{:S(2)}, u32[]{:S(2)}) collective-permute-start(f32[288,1536]{1,0:T(8,128)} %get-tuple-element.54), channel_id=1, source_target_pairs={{0,2},{1,3},{2,0},{3,1},{4,6},{5,7},{6,4},{7,5},{8,10},{9,11},{10,... | collective-permute-start | bytes 5308424 | tf_op jit(solution)/shard_map/ppermute | solution.py:18
  1130.4 73.5 %collective-permute-start.79 = (f32[288,1536]{1,0:T(8,128)}, f32[288,1536]{1,0:T(8,128)}, u32[]{:S(2)}, u32[]{:S(2)}) collective-permute-start(f32[288,1536]{1,0:T(8,128)} %get-tuple-element.58), channel_id=1, source_target_pairs={{0,2},{1,3},{2,0},{3,1},{4,6},{5,7},{6,4},{7,5},{8,10},{9,11},{10,... | collective-permute-start | bytes 5308424 | tf_op jit(solution)/shard_map/ppermute | solution.py:18
  (124 other events, 3054.1 us)
